TPU v7x, 128 devices: a whole 4x4x4 slice. The times are simulated.
128 devices in a mesh: row: 8 (over z, y_hi), col: 16 (over x, y_lo, core).
Axes of the slice: x: 4, y: 4 (y_hi: 2, y_lo: 2; y = y_hi * 2 + y_lo), z: 4, core: 2. Of those that a mesh axis runs over, the one named last changes fastest.
Arguments:
- tri_panels: float32 [8192, 8192], P('row', 'col'), may hold values from -1 to 2, as said below
- rhs_rows: float32 [8192, 2048], P(('row', 'col')), may hold values from -6 to 6
Outputs:
- rhs_grid: float32 [8192, 2048], P('row', 'col')
Inputs may be any that keep to these rules, and one draw needn't show every extreme that they name: `tri_panels`: in L's row order the entries above the diagonal are zero and the diagonal entries are positive.
All inputs are finite; a program needn't handle non-finite values.
Results may differ from a plain program's by a relative error of at most 0.00011.
Values sent between devices are 32-bit elements; how exact they have to be, the bound alone decides.
No kernel may reach another device: no remote copies, remote signals or barrier semaphores. Data moves between devices by JAX's collectives and lax.ppermute only.
A program may use at most 256 MiB of HBM per device.

v0:
```python
import jax
import jax.numpy as jnp
from jax import lax
from jax.experimental import pallas as pl
from jax.experimental.pallas import tpu as pltpu
from jax.sharding import PartitionSpec as P

F32 = jnp.float32
BF16 = jnp.bfloat16
VMEM = pltpu.VMEM
SMEM = pltpu.SMEM
TILE = 256

def split(x):
    hi = x.astype(BF16)
    lo = (x - hi.astype(F32)).astype(BF16)
    return hi, lo


def left3(x):
    hi, lo = split(x)
    return jnp.concatenate([hi, hi, lo], 1)


def right3(x):
    hi, lo = split(x)
    return jnp.concatenate([hi, lo, hi], 0)


def mm3(a, b):
    return jnp.dot(left3(a), right3(b), preferred_element_type=F32)


def wide(x):
    return jnp.concatenate(split(x), 1)


def mmw(hi, lo, w):
    r = jnp.dot(hi, w, preferred_element_type=F32) + jnp.dot(lo, w, preferred_element_type=F32)
    n = w.shape[1] // 2
    return r[:, :n] + r[:, n:]


def vspec():
    return pl.BlockSpec(memory_space=VMEM)


def sspec():
    return pl.BlockSpec(memory_space=SMEM)


def aspec():
    return pl.BlockSpec(memory_space=pl.ANY)


def params(mib):
    return pltpu.CompilerParams(vmem_limit_bytes=mib * 1024 * 1024)


def rows_loop(n, body, tile=TILE):
    lax.fori_loop(0, n // tile, lambda r, _: (body(pl.ds(pl.multiple_of(r * tile, tile), tile)), 0)[1], 0)


def inverse_kernel(flag, own, out):
    nb = own.shape[1]
    h = nb // 2
    out[...] = own[...]

    def invert(slot):
        row = lax.broadcasted_iota(jnp.int32, (h, h), 0)
        col = lax.broadcasted_iota(jnp.int32, (h, h), 1)
        a0 = own[slot, :h, :h]
        a1 = own[slot, h:, h:]
        on = row == col
        y0 = jnp.where(on, 1.0 / jnp.where(on, a0, 1.0), 0.0)
        y1 = jnp.where(on, 1.0 / jnp.where(on, a1, 1.0), 0.0)

        def level(n, ys):
            y0, y1 = ys
            s = lax.shift_left(jnp.int32(1), n)
            pick = (lax.shift_right_logical(row, n + 1) == lax.shift_right_logical(col, n + 1))
            pick = pick & ((row & s) != 0) & ((col & s) == 0)
            e0 = jnp.where(pick, a0, 0.0)
            e1 = jnp.where(pick, a1, 0.0)
            z0 = mm3(e0, y0)
            z1 = mm3(e1, y1)
            return y0 - mm3(y0, z0), y1 - mm3(y1, z1)

        steps = h.bit_length() - 1
        y0, y1 = lax.fori_loop(0, steps, level, (y0, y1))
        z = mm3(own[slot, h:, :h], y0)
        out[slot, :h, :h] = y0
        out[slot, h:, h:] = y1
        out[slot, h:, :h] = -mm3(y1, z)
        out[slot, :h, h:] = jnp.zeros((h, h), F32)

    @pl.when(flag[0] > 0)
    def _():
        invert(flag[1])


def inverse_call(flag, own):
    return pl.pallas_call(
        inverse_kernel,
        out_shape=jax.ShapeDtypeStruct(own.shape, F32),
        in_specs=[sspec(), vspec()],
        out_specs=vspec(),
        compiler_params=params(20),
        name="inverse",
    )(flag, own)


def load_call(g):
    parts, count, rows, nb = g.shape

    def kernel(g, hi, lo):
        k = pl.program_id(0)
        for part in range(parts):
            for at in range(0, rows, 128):
                ds = pl.ds(part * rows + at, 128)
                hi[k, ds], lo[k, ds] = split(g[part, 0, at : at + 128])

    out = jax.ShapeDtypeStruct((count, nb, nb), BF16)
    return pl.pallas_call(
        kernel,
        out_shape=(out, out),
        grid=(count,),
        in_specs=[pl.BlockSpec((parts, 1, rows, nb), lambda k: (0, k, 0, 0))],
        out_specs=(vspec(), vspec()),
        compiler_params=params(6),
        name="load",
    )(g)


def prep_call(tab, base, hi, lo, acc):
    nb, width = acc.shape

    def kernel(tab, hi, lo, acc, nearh, nearl, cur):
        ki = tab[base]
        kn = tab[base + 1]
        w = jnp.concatenate([hi[kn], lo[kn]], 1)
        a = wide(acc[...])

        def mul(ds):
            nearh[ds], nearl[ds] = split(mmw(hi[ki, ds], lo[ki, ds], w))
            cur[ds] = mmw(hi[ki, ds], lo[ki, ds], a)

        rows_loop(nb, mul)

    sq = jax.ShapeDtypeStruct((nb, nb), BF16)
    return pl.pallas_call(
        kernel,
        out_shape=(sq, sq, jax.ShapeDtypeStruct((nb, width), F32)),
        in_specs=[sspec()] + [vspec()] * 3,
        out_specs=(vspec(),) * 3,
        compiler_params=params(8),
        name="prep",
    )(tab, hi, lo, acc)


ROW = 8


def near_call(tab, tok, nearh, nearl, got, cur, mine, store):
    keep = store is not None

    def kernel(tab, tok, nearh, nearl, got, cur, mine, *rest):
        out, tok_out = rest[-2:]
        at = tok[0] * ROW
        tok_out[0] = tok[0] + 1

        @pl.when(tab[at + 6] > 0)
        def _():
            w = wide(got[...])

            def mul(ds):
                out[ds] = cur[ds] - mmw(nearh[ds], nearl[ds], w)

            rows_loop(out.shape[0], mul)
            if keep:
                k = tab[at + 7]
                rest[1][k] = got[...]
                rest[1][k + 1] = out[...]

        @pl.when(tab[at + 6] == 0)
        def _():
            out[...] = mine[...]

    outs = [jax.ShapeDtypeStruct(mine.shape, F32), jax.ShapeDtypeStruct((1,), jnp.int32)]
    ospecs = [vspec(), sspec()]
    args = [tab, tok, nearh, nearl, got, cur, mine]
    if keep:
        outs.insert(0, jax.ShapeDtypeStruct(store.shape, F32))
        ospecs.insert(0, vspec())
        args.append(store)
    res = pl.pallas_call(
        kernel,
        out_shape=tuple(outs),
        in_specs=[sspec(), sspec()] + [vspec()] * (len(args) - 2),
        out_specs=tuple(ospecs),
        input_output_aliases={7: 0} if keep else {},
        compiler_params=params(4),
        name="near",
    )(*args)
    return res if keep else (None,) + tuple(res)


def far_call(tab, tok, hi, lo, acc, cur, xb, xa, store):
    nb = acc.shape[0]
    keep = store is not None

    def kernel(tab, tok, hi, lo, acc, cur, xb, xa, *rest):
        acc_out, cur_out = rest[-2:]
        at = (tok[0] - 1) * ROW

        @pl.when(tab[at + 2] > 0)
        def _():
            kb = tab[at + 0]
            ka = tab[at + 1]
            ki = tab[at + 5]
            wb = wide(xb[...])
            wa = wide(xa[...])

            def mul(ds):
                acc_out[ds] = acc[ds] - (mmw(hi[kb, ds], lo[kb, ds], wb) + mmw(hi[ka, ds], lo[ka, ds], wa))

            rows_loop(nb, mul)
            a = wide(acc_out[...])

            def mul2(ds):
                cur_out[ds] = mmw(hi[ki, ds], lo[ki, ds], a)

            rows_loop(nb, mul2)
            if keep:
                rest[1][tab[at + 3]] = xb[...]
                rest[1][tab[at + 4]] = xa[...]

    out = jax.ShapeDtypeStruct(acc.shape, F32)
    outs = [out, out]
    args = [tab, tok, hi, lo, acc, cur, xb, xa]
    alias = {4: 0, 5: 1}
    if keep:
        outs.insert(0, jax.ShapeDtypeStruct(store.shape, F32))
        args.append(store)
        alias = {8: 0, 4: 1, 5: 2}
    res = pl.pallas_call(
        kernel,
        out_shape=tuple(outs),
        in_specs=[sspec(), sspec()] + [vspec()] * (len(args) - 2),
        out_specs=(vspec(),) * len(outs),
        input_output_aliases=alias,
        compiler_params=params(4),
        name="far",
    )(*args)
    return res if keep else (None,) + tuple(res)


def bulk_call(tab, row, hi, lo, store, acc, xb, xa, count):
    nb, width = acc.shape

    def kernel(tab, hi, lo, store, acc, xb, xa, out, last):
        out[...] = acc[...]

        def one(k, _):
            last[...] = store[k]

            @pl.when((tab[row * ROW + 2] > 0) & (tab[row * ROW + 3] == k))
            def _():
                last[...] = xb[...]

            @pl.when((tab[row * ROW + 2] > 0) & (tab[row * ROW + 4] == k))
            def _():
                last[...] = xa[...]

            w = wide(last[...])

            def mul(ds):
                out[ds] = out[ds] - mmw(hi[k, ds], lo[k, ds], w)

            rows_loop(nb, mul)
            return 0

        lax.fori_loop(0, count, one, 0)

    return pl.pallas_call(
        kernel,
        out_shape=jax.ShapeDtypeStruct(acc.shape, F32),
        in_specs=[sspec()] + [vspec()] * 6,
        out_specs=vspec(),
        scratch_shapes=[VMEM((nb, width), F32)],
        compiler_params=params(4),
        name="bulk",
    )(tab, hi, lo, store, acc, xb, xa)


def after(x, *others):
    return lax.optimization_barrier((x,) + others)[0]


def on_device(tri_panels, rhs_rows):
    R = lax.axis_size("row")
    C = lax.axis_size("col")
    p = lax.axis_index("row")
    c = lax.axis_index("col")
    nb = tri_panels.shape[1]
    half = nb // 2
    blocks = tri_panels.shape[0] // nb
    sub = nb // C
    width = rhs_rows.shape[1] // C

    def ints(*v):
        return jnp.stack([jnp.asarray(x, jnp.int32) for x in v])

    own = tri_panels.reshape(blocks, nb, nb)
    flag = ints(c % R == p, c // R)
    own = inverse_call(flag, own)
    top, low = own[0], own[1]
    moved = lax.ppermute(top[half:], "col", [(i, i + R) for i in range(R)])
    u0 = jnp.where(c < R, top[:half], moved)

    g0 = lax.all_gather(u0, "col", axis=0, tiled=False).reshape(2, R, half, nb)
    g1 = lax.all_gather(low, "col", axis=0, tiled=False).reshape(1, C, nb, nb)

    parted = rhs_rows.reshape(blocks * sub, C, width).transpose(1, 0, 2)
    got = lax.all_to_all(parted, "col", split_axis=0, concat_axis=0, tiled=False)
    state = got.reshape(C, blocks, sub, width).transpose(1, 0, 2, 3).reshape(blocks, nb, width)
    acc, acc1 = state[0], state[1]

    rows = []
    for t in range(C - 1):
        q = (p - t) % R
        i = t + q
        kA = i - 2 * q + 1
        kB = kA + 1
        inwin = (q >= 2) & (q <= 4)
        first = t + 1 < R
        top_k = R - 1 if first else C - 1
        rows += [
            jnp.clip(kB, 0, top_k),
            jnp.clip(kA, 0, top_k),
            inwin,
            jnp.where(kB >= 0, jnp.minimum(kB, R), R),
            jnp.where(kA >= 0, jnp.minimum(kA, R), R),
            p if first else R + p,
            p == (t + 1) % R,
            min(t, R - 1),
        ]
    tab = ints(*rows, p, jnp.maximum(p - 1, 0), R + p, R + p - 1)
    hi, lo = load_call(g0)
    nearh, nearl, cur = prep_call(tab, (C - 1) * ROW, hi, lo, acc)
    zero = jnp.zeros((nb, width), F32)
    mine = jnp.where(p == 0, cur, zero)
    store = jnp.zeros((R + 1, nb, width), F32)
    store = lax.dynamic_update_index_in_dim(store, mine, 0, 0)
    tok = jnp.zeros((1,), jnp.int32)
    for t in range(C - 1):
        s = t % R
        with jax.named_scope(f"near{t}"):
            P1 = lax.ppermute(mine, "row", [(s, (s + 1) % R)])
        B = [((t - j) % R, (t + 2 + j) % R) for j in range(3) if t - j >= 0 and t + 2 + j < C]
        A = [((t - j) % R, (t + 1 + j) % R) for j in range(1, 4) if t - j >= 0 and t + 1 + j < C]
        with jax.named_scope(f"far{t}"):
            XB = lax.ppermute(mine, "row", B) if B else zero
            XA = lax.ppermute(mine, "row", A) if A else zero
        first = t + 1 < R
        store, mine, tok = near_call(tab, tok, nearh, nearl, P1, cur, mine, store if first else None)
        if first:
            out0 = mine
        if t + 1 == R - 1:
            hi, lo = load_call(g1)
            acc = bulk_call(tab, t, hi, lo, store, acc1, XB, XA, R)
            nearh, nearl, cur = prep_call(tab, (C - 1) * ROW + 2, hi, lo, acc)
        elif B or A:
            store, acc, cur = far_call(tab, tok, hi, lo, acc, cur, XB, XA, store if first else None)
    return jnp.concatenate([out0, mine], 0)


def solution(mesh):
    return jax.shard_map(
        on_device,
        mesh=mesh,
        in_specs=(P("row", "col"), P(("row", "col"), None)),
        out_specs=P("row", "col"),
        check_vma=False,
    )
```

profile of v0, /device:TPU:120, one launch (start us, length us, event | category | flops | bytes accessed | tf_op | source)
XLA Modules:
  0.0 315.9 jit_solution(8868160509247644957)
XLA Ops:
  6.6 1.6 copy-done.2
  9.7 4.9 %collective-permute-start = (f32[256,512]{1,0:T(8,128)}, f32[256,512]{1,0:T(8,128)S(1)}, u32[]{:S(2)}, u32[]{:S(2)}) collective-permute-start(f32[256,512]{1,0:T(8,128)} %slice_bitcast_fusion), channel_id=1, source_target_pairs={{0,8},{1,9},{2,10},{3,11},{4,12},{5,13},{6,14},{7,15},{16,24},{17,... | collective-permute-start | bytes 1572872 | tf_op jit(solution)/shard_map/ppermute | solution.py:318
  14.7 11.4 %collective-permute-done = f32[256,512]{1,0:T(8,128)S(1)} collective-permute-done((f32[256,512]{1,0:T(8,128)}, f32[256,512]{1,0:T(8,128)S(1)}, u32[]{:S(2)}, u32[]{:S(2)}) %collective-permute-start) | collective-permute-done | bytes 524320 | tf_op jit(solution)/shard_map/ppermute | solution.py:318
  29.2 7.4 %all-to-all-start = ((f32[16,64,128]{2,1,0:T(8,128)}), f32[16,64,128]{2,1,0:T(8,128)S(1)}, u32[]{:S(2)}, u32[]{:S(2)}) async-start(f32[16,64,128]{2,1,0:T(8,128)} %copy.43), calls=%async_computation | async-start | bytes 1048576 | tf_op jit(solution)/shard_map/all_to_all | solution.py:325
  36.9 12.0 %all-to-all-done = f32[16,64,128]{2,1,0:T(8,128)S(1)} async-done(((f32[16,64,128]{2,1,0:T(8,128)}), f32[16,64,128]{2,1,0:T(8,128)S(1)}, u32[]{:S(2)}, u32[]{:S(2)}) %all-to-all-start) | async-done | bytes 524320 | tf_op jit(solution)/shard_map/all_to_all | solution.py:325
  48.9 37.0 %all-gather.6.cloned.1.call-done = f32[4096,512]{1,0:T(8,128)} async-done(((f32[256,512]{1,0:T(8,128)}), f32[4096,512]{1,0:T(8,128)}) %all-gather.6.cloned.1.call-update) | async-done | bytes 8388624 | tf_op jit(solution)/shard_map/all_gather | solution.py:321
  85.9 3.4 %copy-done.1 = f32[4096,512]{1,0:T(8,128)S(1)} copy-done((f32[4096,512]{1,0:T(8,128)S(1)}, f32[4096,512]{1,0:T(8,128)}, u32[]{:S(2)}) %copy-start.1) | copy-done | bytes 8388632
  89.3 2.0 load.2
  91.3 2.4 prep.2
  99.7 1.7 near.16
  104.7 1.7 near.17
  111.0 1.7 near.18
  116.0 30.7 %collective-permute-done.12.xa = f32[512,128]{1,0:T(8,128)S(1)} collective-permute-done((f32[512,128]{1,0:T(8,128)S(1)}, f32[512,128]{1,0:T(8,128)S(1)}, u32[]{:S(2)}, u32[]{:S(2)}) %collective-permute-start.12) | collective-permute-done | bytes 262176 | tf_op jit(solution)/shard_map/far3/ppermute | solution.py:364
  146.7 2.8 far.16
  149.6 1.7 near.19
  154.6 17.3 %collective-permute-done.15.xa = f32[512,128]{1,0:T(8,128)S(1)} collective-permute-done((f32[512,128]{1,0:T(8,128)S(1)}, f32[512,128]{1,0:T(8,128)S(1)}, u32[]{:S(2)}, u32[]{:S(2)}) %collective-permute-start.15) | collective-permute-done | bytes 262176 | tf_op jit(solution)/shard_map/far4/ppermute | solution.py:364
  171.9 6.0 %collective-permute-done.14.xb = f32[512,128]{1,0:T(8,128)S(1)} collective-permute-done((f32[512,128]{1,0:T(8,128)S(1)}, f32[512,128]{1,0:T(8,128)S(1)}, u32[]{:S(2)}, u32[]{:S(2)}) %collective-permute-start.14) | collective-permute-done | bytes 262176 | tf_op jit(solution)/shard_map/far4/ppermute | solution.py:363
  177.9 2.8 far.17
  180.8 1.9 near.20
  185.4 5.4 %collective-permute-done.18.xa = f32[512,128]{1,0:T(8,128)S(1)} collective-permute-done((f32[512,128]{1,0:T(8,128)S(1)}, f32[512,128]{1,0:T(8,128)S(1)}, u32[]{:S(2)}, u32[]{:S(2)}) %collective-permute-start.18) | collective-permute-done | bytes 262176 | tf_op jit(solution)/shard_map/far5/ppermute | solution.py:364
  190.8 9.2 %collective-permute-done.17.xb = f32[512,128]{1,0:T(8,128)S(1)} collective-permute-done((f32[512,128]{1,0:T(8,128)S(1)}, f32[512,128]{1,0:T(8,128)S(1)}, u32[]{:S(2)}, u32[]{:S(2)}) %collective-permute-start.17) | collective-permute-done | bytes 262176 | tf_op jit(solution)/shard_map/far5/ppermute | solution.py:363
  200.0 2.9 far.18
  202.8 2.8 near.21
  205.6 2.0 collective-permute-start.21
  209.0 2.2 collective-permute-start.23
  211.1 5.8 %copy-done = f32[16,512,512]{2,1,0:T(8,128)S(1)} copy-done((f32[16,512,512]{2,1,0:T(8,128)S(1)}, f32[16,512,512]{2,1,0:T(8,128)}, u32[]{:S(2)}) %copy-start) | copy-done | bytes 16777240
  216.9 2.8 load.3
  219.7 5.9 %bulk.1.acc = f32[512,128]{1,0:T(8,128)S(1)} custom-call(s32[124]{0:T(128)S(1)} %stack.477.tab, bf16[16,512,512]{2,1,0:T(8,128)(2,1)S(1)} %get-tuple-element.123.hi, bf16[16,512,512]{2,1,0:T(8,128)(2,1)S(1)} %get-tuple-element.124.lo, f32[9,512,128]{2,1,0:T(8,128)S(1)} %get-tuple-element.125.store, f32[512,128]{1,0:T(8,128)S(1)} %bitcast.114, ...), custom_call_target="tpu_custom_call" | custom-call | tf_op jit(solution)/shard_map/bulk/pallas_call | solution.py:285
  225.6 2.4 prep.3
  228.1 2.2 near.22
  233.6 1.7 far.19
  235.3 1.7 near.23
  240.4 5.1 %collective-permute-done.26.xb = f32[512,128]{1,0:T(8,128)S(1)} collective-permute-done((f32[512,128]{1,0:T(8,128)S(1)}, f32[512,128]{1,0:T(8,128)S(1)}, u32[]{:S(2)}, u32[]{:S(2)}) %collective-permute-start.26) | collective-permute-done | bytes 262176 | tf_op jit(solution)/shard_map/far8/ppermute | solution.py:363
  246.6 1.7 near.24
  252.3 1.7 near.25
  258.5 1.7 near.26
  263.5 3.0 collective-permute-done.36.xa
  266.6 5.0 %collective-permute-done.35.xb = f32[512,128]{1,0:T(8,128)S(1)} collective-permute-done((f32[512,128]{1,0:T(8,128)S(1)}, f32[512,128]{1,0:T(8,128)S(1)}, u32[]{:S(2)}, u32[]{:S(2)}) %collective-permute-start.35) | collective-permute-done | bytes 262176 | tf_op jit(solution)/shard_map/far11/ppermute | solution.py:363
  271.6 2.8 far.23
  274.4 1.7 near.27
  279.5 4.5 %collective-permute-done.39.xa = f32[512,128]{1,0:T(8,128)S(1)} collective-permute-done((f32[512,128]{1,0:T(8,128)S(1)}, f32[512,128]{1,0:T(8,128)S(1)}, u32[]{:S(2)}, u32[]{:S(2)}) %collective-permute-start.39) | collective-permute-done | bytes 262176 | tf_op jit(solution)/shard_map/far12/ppermute | solution.py:364
  284.7 2.8 far.24
  287.6 1.7 near.28
  290.6 3.5 %collective-permute-done.42.xa = f32[512,128]{1,0:T(8,128)S(1)} collective-permute-done((f32[512,128]{1,0:T(8,128)S(1)}, f32[512,128]{1,0:T(8,128)S(1)}, u32[]{:S(2)}, u32[]{:S(2)}) %collective-permute-start.42) | collective-permute-done | bytes 262176 | tf_op jit(solution)/shard_map/far13/ppermute | solution.py:364
  294.1 3.0 collective-permute-done.41.xb
  297.1 2.8 far.25
  299.9 6.0 %collective-permute-done.40.got = f32[512,128]{1,0:T(8,128)S(1)} collective-permute-done((f32[512,128]{1,0:T(8,128)S(1)}, f32[512,128]{1,0:T(8,128)S(1)}, u32[]{:S(2)}, u32[]{:S(2)}) %collective-permute-start.40) | collective-permute-done | bytes 262176 | tf_op jit(solution)/shard_map/near14/ppermute | solution.py:359
  305.9 2.4 near.29
  (101 shorter events, 54.6 us)
Async XLA Ops:
  6.5 79.4 %all-gather.6.cloned.1.call-start = ((), (), s32[]{:S(2)}) async-start(), calls=%async_computation.2 | async-start | bytes 8912896 | tf_op jit(solution)/shard_map/all_gather | solution.py:321
  9.7 16.4 %collective-permute-start = (f32[256,512]{1,0:T(8,128)}, f32[256,512]{1,0:T(8,128)S(1)}, u32[]{:S(2)}, u32[]{:S(2)}) collective-permute-start(f32[256,512]{1,0:T(8,128)} %slice_bitcast_fusion), channel_id=1, source_target_pairs={{0,8},{1,9},{2,10},{3,11},{4,12},{5,13},{6,14},{7,15},{16,24},{17,... | collective-permute-start | bytes 1572872 | tf_op jit(solution)/shard_map/ppermute | solution.py:318
  14.7 13.5 %copy-start.3 = (f32[64,2048]{1,0:T(8,128)S(1)}, f32[64,2048]{1,0:T(8,128)}, u32[]{:S(2)}) copy-start(f32[64,2048]{1,0:T(8,128)} %param.3) | copy-start | bytes 1572868
  27.0 184.1 %all-gather.4.cloned.1.call-start = ((), (), s32[]{:S(2)}) async-start(), calls=%async_computation.1 | async-start | bytes 17825792 | tf_op jit(solution)/shard_map/all_gather | solution.py:322
  29.2 19.7 %all-to-all-start = ((f32[16,64,128]{2,1,0:T(8,128)}), f32[16,64,128]{2,1,0:T(8,128)S(1)}, u32[]{:S(2)}, u32[]{:S(2)}) async-start(f32[16,64,128]{2,1,0:T(8,128)} %copy.43), calls=%async_computation | async-start | bytes 1048576 | tf_op jit(solution)/shard_map/all_to_all | solution.py:325
  93.7 1.6 collective-permute-start.1
  94.4 4.1 %collective-permute-start.3 = (f32[512,128]{1,0:T(8,128)S(1)}, f32[512,128]{1,0:T(8,128)S(1)}, u32[]{:S(2)}, u32[]{:S(2)}) collective-permute-start(f32[512,128]{1,0:T(8,128)S(1)} %broadcast_select_fusion.mine), channel_id=1, source_target_pairs={{0,32},{1,33},{2,34},{3,35},{4,36},{5,37},{6,38},{7,39},{8,40},{9,... | collective-permute-start | bytes 786440 | tf_op jit(solution)/shard_map/far0/ppermute | solution.py:363
  96.4 3.3 %collective-permute-start.2 = (f32[512,128]{1,0:T(8,128)S(1)}, f32[512,128]{1,0:T(8,128)S(1)}, u32[]{:S(2)}, u32[]{:S(2)}) collective-permute-start(f32[512,128]{1,0:T(8,128)S(1)} %get-tuple-element.87.mine), channel_id=1, source_target_pairs={{16,32},{17,33},{18,34},{19,35},{20,36},{21,37},{22,38},{23,39},{2... | collective-permute-start | bytes 786440 | tf_op jit(solution)/shard_map/near1/ppermute | solution.py:359
  97.1 6.4 %collective-permute-start.6 = (f32[512,128]{1,0:T(8,128)S(1)}, f32[512,128]{1,0:T(8,128)S(1)}, u32[]{:S(2)}, u32[]{:S(2)}) collective-permute-start(f32[512,128]{1,0:T(8,128)S(1)} %get-tuple-element.87.mine), channel_id=1, source_target_pairs={{0,48},{1,49},{2,50},{3,51},{4,52},{5,53},{6,54},{7,55},{8,56},{9,... | collective-permute-start | bytes 786440 | tf_op jit(solution)/shard_map/far1/ppermute | solution.py:364
  97.8 5.7 %collective-permute-start.5 = (f32[512,128]{1,0:T(8,128)S(1)}, f32[512,128]{1,0:T(8,128)S(1)}, u32[]{:S(2)}, u32[]{:S(2)}) collective-permute-start(f32[512,128]{1,0:T(8,128)S(1)} %get-tuple-element.87.mine), channel_id=1, source_target_pairs={{16,48},{0,64},{17,49},{1,65},{18,50},{2,66},{19,51},{3,67},{20,52... | collective-permute-start | bytes 786440 | tf_op jit(solution)/shard_map/far1/ppermute | solution.py:363
  101.5 3.3 %collective-permute-start.4 = (f32[512,128]{1,0:T(8,128)S(1)}, f32[512,128]{1,0:T(8,128)S(1)}, u32[]{:S(2)}, u32[]{:S(2)}) collective-permute-start(f32[512,128]{1,0:T(8,128)S(1)} %get-tuple-element.92.mine), channel_id=1, source_target_pairs={{32,48},{33,49},{34,50},{35,51},{36,52},{37,53},{38,54},{39,55},{4... | collective-permute-start | bytes 786440 | tf_op jit(solution)/shard_map/near2/ppermute | solution.py:359
  102.1 7.6 %collective-permute-start.9 = (f32[512,128]{1,0:T(8,128)S(1)}, f32[512,128]{1,0:T(8,128)S(1)}, u32[]{:S(2)}, u32[]{:S(2)}) collective-permute-start(f32[512,128]{1,0:T(8,128)S(1)} %get-tuple-element.92.mine), channel_id=1, source_target_pairs={{16,64},{0,80},{17,65},{1,81},{18,66},{2,82},{19,67},{3,83},{20,68... | collective-permute-start | bytes 786440 | tf_op jit(solution)/shard_map/far2/ppermute | solution.py:364
  102.8 6.9 %collective-permute-start.8 = (f32[512,128]{1,0:T(8,128)S(1)}, f32[512,128]{1,0:T(8,128)S(1)}, u32[]{:S(2)}, u32[]{:S(2)}) collective-permute-start(f32[512,128]{1,0:T(8,128)S(1)} %get-tuple-element.92.mine), channel_id=1, source_target_pairs={{32,64},{16,80},{0,96},{33,65},{17,81},{1,97},{34,66},{18,82},{2,9... | collective-permute-start | bytes 786440 | tf_op jit(solution)/shard_map/far2/ppermute | solution.py:363
  106.5 4.5 %collective-permute-start.7 = (f32[512,128]{1,0:T(8,128)S(1)}, f32[512,128]{1,0:T(8,128)S(1)}, u32[]{:S(2)}, u32[]{:S(2)}) collective-permute-start(f32[512,128]{1,0:T(8,128)S(1)} %get-tuple-element.98.mine), channel_id=1, source_target_pairs={{48,64},{49,65},{50,66},{51,67},{52,68},{53,69},{54,70},{55,71},{5... | collective-permute-start | bytes 786440 | tf_op jit(solution)/shard_map/near3/ppermute | solution.py:359
  107.1 39.6 %collective-permute-start.12 = (f32[512,128]{1,0:T(8,128)S(1)}, f32[512,128]{1,0:T(8,128)S(1)}, u32[]{:S(2)}, u32[]{:S(2)}) collective-permute-start(f32[512,128]{1,0:T(8,128)S(1)} %get-tuple-element.98.mine), channel_id=1, source_target_pairs={{32,80},{16,96},{0,112},{33,81},{17,97},{1,113},{34,82},{18,98},{2... | collective-permute-start | bytes 786440 | tf_op jit(solution)/shard_map/far3/ppermute | solution.py:364
  108.4 38.3 %collective-permute-start.11 = (f32[512,128]{1,0:T(8,128)S(1)}, f32[512,128]{1,0:T(8,128)S(1)}, u32[]{:S(2)}, u32[]{:S(2)}) collective-permute-start(f32[512,128]{1,0:T(8,128)S(1)} %get-tuple-element.98.mine), channel_id=1, source_target_pairs={{48,80},{32,96},{16,112},{49,81},{33,97},{17,113},{50,82},{34,98},... | collective-permute-start | bytes 786440 | tf_op jit(solution)/shard_map/far3/ppermute | solution.py:363
  112.7 36.9 %collective-permute-start.10 = (f32[512,128]{1,0:T(8,128)S(1)}, f32[512,128]{1,0:T(8,128)S(1)}, u32[]{:S(2)}, u32[]{:S(2)}) collective-permute-start(f32[512,128]{1,0:T(8,128)S(1)} %get-tuple-element.104.mine), channel_id=1, source_target_pairs={{64,80},{65,81},{66,82},{67,83},{68,84},{69,85},{70,86},{71,87},{7... | collective-permute-start | bytes 786440 | tf_op jit(solution)/shard_map/near4/ppermute | solution.py:359
  113.4 58.5 %collective-permute-start.15 = (f32[512,128]{1,0:T(8,128)S(1)}, f32[512,128]{1,0:T(8,128)S(1)}, u32[]{:S(2)}, u32[]{:S(2)}) collective-permute-start(f32[512,128]{1,0:T(8,128)S(1)} %get-tuple-element.104.mine), channel_id=1, source_target_pairs={{48,96},{32,112},{16,0},{49,97},{33,113},{17,1},{50,98},{34,114},{... | collective-permute-start | bytes 786440 | tf_op jit(solution)/shard_map/far4/ppermute | solution.py:364
  114.7 63.2 %collective-permute-start.14 = (f32[512,128]{1,0:T(8,128)S(1)}, f32[512,128]{1,0:T(8,128)S(1)}, u32[]{:S(2)}, u32[]{:S(2)}) collective-permute-start(f32[512,128]{1,0:T(8,128)S(1)} %get-tuple-element.104.mine), channel_id=1, source_target_pairs={{64,96},{48,112},{32,0},{65,97},{49,113},{33,1},{66,98},{50,114},{... | collective-permute-start | bytes 786440 | tf_op jit(solution)/shard_map/far4/ppermute | solution.py:363
  151.3 29.4 %collective-permute-start.13 = (f32[512,128]{1,0:T(8,128)S(1)}, f32[512,128]{1,0:T(8,128)S(1)}, u32[]{:S(2)}, u32[]{:S(2)}) collective-permute-start(f32[512,128]{1,0:T(8,128)S(1)} %get-tuple-element.110.mine), channel_id=1, source_target_pairs={{80,96},{81,97},{82,98},{83,99},{84,100},{85,101},{86,102},{87,103... | collective-permute-start | bytes 786440 | tf_op jit(solution)/shard_map/near5/ppermute | solution.py:359
  152.0 38.8 %collective-permute-start.18 = (f32[512,128]{1,0:T(8,128)S(1)}, f32[512,128]{1,0:T(8,128)S(1)}, u32[]{:S(2)}, u32[]{:S(2)}) collective-permute-start(f32[512,128]{1,0:T(8,128)S(1)} %get-tuple-element.110.mine), channel_id=1, source_target_pairs={{64,112},{48,0},{32,16},{65,113},{49,1},{33,17},{66,114},{50,2},{3... | collective-permute-start | bytes 786440 | tf_op jit(solution)/shard_map/far5/ppermute | solution.py:364
  153.3 46.6 %collective-permute-start.17 = (f32[512,128]{1,0:T(8,128)S(1)}, f32[512,128]{1,0:T(8,128)S(1)}, u32[]{:S(2)}, u32[]{:S(2)}) collective-permute-start(f32[512,128]{1,0:T(8,128)S(1)} %get-tuple-element.110.mine), channel_id=1, source_target_pairs={{80,112},{64,0},{48,16},{81,113},{65,1},{49,17},{82,114},{66,2},{5... | collective-permute-start | bytes 786440 | tf_op jit(solution)/shard_map/far5/ppermute | solution.py:363
  182.7 20.1 %collective-permute-start.16 = (f32[512,128]{1,0:T(8,128)}, f32[512,128]{1,0:T(8,128)S(1)}, u32[]{:S(2)}, u32[]{:S(2)}) collective-permute-start(f32[512,128]{1,0:T(8,128)} %get-tuple-element.116.mine), channel_id=1, source_target_pairs={{96,112},{97,113},{98,114},{99,115},{100,116},{101,117},{102,118},... | collective-permute-start | bytes 786440 | tf_op jit(solution)/shard_map/near6/ppermute | solution.py:359
  184.0 35.7 %collective-permute-start.20 = (f32[512,128]{1,0:T(8,128)}, f32[512,128]{1,0:T(8,128)S(1)}, u32[]{:S(2)}, u32[]{:S(2)}) collective-permute-start(f32[512,128]{1,0:T(8,128)} %get-tuple-element.116.mine), channel_id=1, source_target_pairs={{80,0},{64,16},{48,32},{81,1},{65,17},{49,33},{82,2},{66,18},{50,3... | collective-permute-start | bytes 786440 | tf_op jit(solution)/shard_map/far6/ppermute | solution.py:364
  184.7 35.0 %collective-permute-start.19 = (f32[512,128]{1,0:T(8,128)}, f32[512,128]{1,0:T(8,128)S(1)}, u32[]{:S(2)}, u32[]{:S(2)}) collective-permute-start(f32[512,128]{1,0:T(8,128)} %get-tuple-element.116.mine), channel_id=1, source_target_pairs={{96,0},{80,16},{64,32},{97,1},{81,17},{65,33},{98,2},{82,18},{66,3... | collective-permute-start | bytes 786440 | tf_op jit(solution)/shard_map/far6/ppermute | solution.py:363
  205.6 22.4 %collective-permute-start.21 = (f32[512,128]{1,0:T(8,128)S(1)}, f32[512,128]{1,0:T(8,128)}, u32[]{:S(2)}, u32[]{:S(2)}) collective-permute-start(f32[512,128]{1,0:T(8,128)S(1)} %get-tuple-element.121.mine), channel_id=1, source_target_pairs={{112,0},{113,1},{114,2},{115,3},{116,4},{117,5},{118,6},{119,7},{1... | collective-permute-start | bytes 786440 | tf_op jit(solution)/shard_map/near7/ppermute | solution.py:359
  207.6 25.9 %collective-permute-start.24 = (f32[512,128]{1,0:T(8,128)S(1)}, f32[512,128]{1,0:T(8,128)}, u32[]{:S(2)}, u32[]{:S(2)}) collective-permute-start(f32[512,128]{1,0:T(8,128)S(1)} %get-tuple-element.121.mine), channel_id=1, source_target_pairs={{96,16},{80,32},{64,48},{97,17},{81,33},{65,49},{98,18},{82,34},{6... | collective-permute-start | bytes 786440 | tf_op jit(solution)/shard_map/far7/ppermute | solution.py:364
  209.0 24.6 %collective-permute-start.23 = (f32[512,128]{1,0:T(8,128)S(1)}, f32[512,128]{1,0:T(8,128)}, u32[]{:S(2)}, u32[]{:S(2)}) collective-permute-start(f32[512,128]{1,0:T(8,128)S(1)} %get-tuple-element.121.mine), channel_id=1, source_target_pairs={{112,16},{96,32},{80,48},{113,17},{97,33},{81,49},{114,18},{98,34}... | collective-permute-start | bytes 786440 | tf_op jit(solution)/shard_map/far7/ppermute | solution.py:363
  211.1 5.8 %copy-start = (f32[16,512,512]{2,1,0:T(8,128)S(1)}, f32[16,512,512]{2,1,0:T(8,128)}, u32[]{:S(2)}) copy-start(f32[16,512,512]{2,1,0:T(8,128)} %all-gather.4.cloned.1.call-done) | copy-start | bytes 50331652
  230.2 5.0 %collective-permute-start.22 = (f32[512,128]{1,0:T(8,128)S(1)}, f32[512,128]{1,0:T(8,128)S(1)}, u32[]{:S(2)}, u32[]{:S(2)}) collective-permute-start(f32[512,128]{1,0:T(8,128)S(1)} %get-tuple-element.130.mine), channel_id=1, source_target_pairs={{0,16},{1,17},{2,18},{3,19},{4,20},{5,21},{6,22},{7,23},{8,24},{9,... | collective-permute-start | bytes 786440 | tf_op jit(solution)/shard_map/near8/ppermute | solution.py:359
  230.9 9.4 %collective-permute-start.27 = (f32[512,128]{1,0:T(8,128)S(1)}, f32[512,128]{1,0:T(8,128)S(1)}, u32[]{:S(2)}, u32[]{:S(2)}) collective-permute-start(f32[512,128]{1,0:T(8,128)S(1)} %get-tuple-element.130.mine), channel_id=1, source_target_pairs={{112,32},{96,48},{80,64},{113,33},{97,49},{81,65},{114,34},{98,50}... | collective-permute-start | bytes 786440 | tf_op jit(solution)/shard_map/far8/ppermute | solution.py:364
  232.2 13.2 %collective-permute-start.26 = (f32[512,128]{1,0:T(8,128)S(1)}, f32[512,128]{1,0:T(8,128)S(1)}, u32[]{:S(2)}, u32[]{:S(2)}) collective-permute-start(f32[512,128]{1,0:T(8,128)S(1)} %get-tuple-element.130.mine), channel_id=1, source_target_pairs={{0,32},{112,48},{96,64},{1,33},{113,49},{97,65},{2,34},{114,50},{9... | collective-permute-start | bytes 786440 | tf_op jit(solution)/shard_map/far8/ppermute | solution.py:363
  237.0 9.6 %collective-permute-start.25 = (f32[512,128]{1,0:T(8,128)S(1)}, f32[512,128]{1,0:T(8,128)S(1)}, u32[]{:S(2)}, u32[]{:S(2)}) collective-permute-start(f32[512,128]{1,0:T(8,128)S(1)} %get-tuple-element.133.mine), channel_id=1, source_target_pairs={{16,32},{17,33},{18,34},{19,35},{20,36},{21,37},{22,38},{23,39},{2... | collective-permute-start | bytes 786440 | tf_op jit(solution)/shard_map/near9/ppermute | solution.py:359
  237.7 13.3 %collective-permute-start.30 = (f32[512,128]{1,0:T(8,128)S(1)}, f32[512,128]{1,0:T(8,128)S(1)}, u32[]{:S(2)}, u32[]{:S(2)}) collective-permute-start(f32[512,128]{1,0:T(8,128)S(1)} %get-tuple-element.133.mine), channel_id=1, source_target_pairs={{0,48},{112,64},{96,80},{1,49},{113,65},{97,81},{2,50},{114,66},{9... | collective-permute-start | bytes 786440 | tf_op jit(solution)/shard_map/far9/ppermute | solution.py:364
  239.0 12.0 %collective-permute-start.29 = (f32[512,128]{1,0:T(8,128)S(1)}, f32[512,128]{1,0:T(8,128)S(1)}, u32[]{:S(2)}, u32[]{:S(2)}) collective-permute-start(f32[512,128]{1,0:T(8,128)S(1)} %get-tuple-element.133.mine), channel_id=1, source_target_pairs={{16,48},{0,64},{112,80},{17,49},{1,65},{113,81},{18,50},{2,66},{11... | collective-permute-start | bytes 786440 | tf_op jit(solution)/shard_map/far9/ppermute | solution.py:363
  248.4 3.9 %collective-permute-start.28 = (f32[512,128]{1,0:T(8,128)S(1)}, f32[512,128]{1,0:T(8,128)S(1)}, u32[]{:S(2)}, u32[]{:S(2)}) collective-permute-start(f32[512,128]{1,0:T(8,128)S(1)} %get-tuple-element.137.mine), channel_id=1, source_target_pairs={{32,48},{33,49},{34,50},{35,51},{36,52},{37,53},{38,54},{39,55},{4... | collective-permute-start | bytes 786440 | tf_op jit(solution)/shard_map/near10/ppermute | solution.py:359
  249.0 8.3 %collective-permute-start.33 = (f32[512,128]{1,0:T(8,128)S(1)}, f32[512,128]{1,0:T(8,128)S(1)}, u32[]{:S(2)}, u32[]{:S(2)}) collective-permute-start(f32[512,128]{1,0:T(8,128)S(1)} %get-tuple-element.137.mine), channel_id=1, source_target_pairs={{16,64},{0,80},{112,96},{17,65},{1,81},{113,97},{18,66},{2,82},{11... | collective-permute-start | bytes 786440 | tf_op jit(solution)/shard_map/far10/ppermute | solution.py:364
  250.4 7.0 %collective-permute-start.32 = (f32[512,128]{1,0:T(8,128)S(1)}, f32[512,128]{1,0:T(8,128)S(1)}, u32[]{:S(2)}, u32[]{:S(2)}) collective-permute-start(f32[512,128]{1,0:T(8,128)S(1)} %get-tuple-element.137.mine), channel_id=1, source_target_pairs={{32,64},{16,80},{0,96},{33,65},{17,81},{1,97},{34,66},{18,82},{2,9... | collective-permute-start | bytes 786440 | tf_op jit(solution)/shard_map/far10/ppermute | solution.py:363
  254.0 4.5 %collective-permute-start.31 = (f32[512,128]{1,0:T(8,128)S(1)}, f32[512,128]{1,0:T(8,128)S(1)}, u32[]{:S(2)}, u32[]{:S(2)}) collective-permute-start(f32[512,128]{1,0:T(8,128)S(1)} %get-tuple-element.141.mine), channel_id=1, source_target_pairs={{48,64},{49,65},{50,66},{51,67},{52,68},{53,69},{54,70},{55,71},{5... | collective-permute-start | bytes 786440 | tf_op jit(solution)/shard_map/near11/ppermute | solution.py:359
  254.7 11.9 %collective-permute-start.36 = (f32[512,128]{1,0:T(8,128)S(1)}, f32[512,128]{1,0:T(8,128)S(1)}, u32[]{:S(2)}, u32[]{:S(2)}) collective-permute-start(f32[512,128]{1,0:T(8,128)S(1)} %get-tuple-element.141.mine), channel_id=1, source_target_pairs={{32,80},{16,96},{0,112},{33,81},{17,97},{1,113},{34,82},{18,98},{2... | collective-permute-start | bytes 786440 | tf_op jit(solution)/shard_map/far11/ppermute | solution.py:364
  256.0 15.6 %collective-permute-start.35 = (f32[512,128]{1,0:T(8,128)S(1)}, f32[512,128]{1,0:T(8,128)S(1)}, u32[]{:S(2)}, u32[]{:S(2)}) collective-permute-start(f32[512,128]{1,0:T(8,128)S(1)} %get-tuple-element.141.mine), channel_id=1, source_target_pairs={{48,80},{32,96},{16,112},{49,81},{33,97},{17,113},{50,82},{34,98},... | collective-permute-start | bytes 786440 | tf_op jit(solution)/shard_map/far11/ppermute | solution.py:363
  260.3 14.2 %collective-permute-start.34 = (f32[512,128]{1,0:T(8,128)S(1)}, f32[512,128]{1,0:T(8,128)S(1)}, u32[]{:S(2)}, u32[]{:S(2)}) collective-permute-start(f32[512,128]{1,0:T(8,128)S(1)} %get-tuple-element.145.mine), channel_id=1, source_target_pairs={{64,80},{65,81},{66,82},{67,83},{68,84},{69,85},{70,86},{71,87},{7... | collective-permute-start | bytes 786440 | tf_op jit(solution)/shard_map/near12/ppermute | solution.py:359
  260.9 23.0 %collective-permute-start.39 = (f32[512,128]{1,0:T(8,128)S(1)}, f32[512,128]{1,0:T(8,128)S(1)}, u32[]{:S(2)}, u32[]{:S(2)}) collective-permute-start(f32[512,128]{1,0:T(8,128)S(1)} %get-tuple-element.145.mine), channel_id=1, source_target_pairs={{48,96},{32,112},{49,97},{33,113},{50,98},{34,114},{51,99},{35,115... | collective-permute-start | bytes 786440 | tf_op jit(solution)/shard_map/far12/ppermute | solution.py:364
  262.2 22.5 %collective-permute-start.38 = (f32[512,128]{1,0:T(8,128)S(1)}, f32[512,128]{1,0:T(8,128)S(1)}, u32[]{:S(2)}, u32[]{:S(2)}) collective-permute-start(f32[512,128]{1,0:T(8,128)S(1)} %get-tuple-element.145.mine), channel_id=1, source_target_pairs={{64,96},{48,112},{65,97},{49,113},{66,98},{50,114},{67,99},{51,115... | collective-permute-start | bytes 786440 | tf_op jit(solution)/shard_map/far12/ppermute | solution.py:363
  276.2 11.4 %collective-permute-start.37 = (f32[512,128]{1,0:T(8,128)S(1)}, f32[512,128]{1,0:T(8,128)S(1)}, u32[]{:S(2)}, u32[]{:S(2)}) collective-permute-start(f32[512,128]{1,0:T(8,128)S(1)} %get-tuple-element.149.mine), channel_id=1, source_target_pairs={{80,96},{81,97},{82,98},{83,99},{84,100},{85,101},{86,102},{87,103... | collective-permute-start | bytes 786440 | tf_op jit(solution)/shard_map/near13/ppermute | solution.py:359
  276.9 17.2 %collective-permute-start.42 = (f32[512,128]{1,0:T(8,128)S(1)}, f32[512,128]{1,0:T(8,128)S(1)}, u32[]{:S(2)}, u32[]{:S(2)}) collective-permute-start(f32[512,128]{1,0:T(8,128)S(1)} %get-tuple-element.149.mine), channel_id=1, source_target_pairs={{64,112},{65,113},{66,114},{67,115},{68,116},{69,117},{70,118},{71... | collective-permute-start | bytes 786440 | tf_op jit(solution)/shard_map/far13/ppermute | solution.py:364
  278.2 18.9 %collective-permute-start.41 = (f32[512,128]{1,0:T(8,128)S(1)}, f32[512,128]{1,0:T(8,128)S(1)}, u32[]{:S(2)}, u32[]{:S(2)}) collective-permute-start(f32[512,128]{1,0:T(8,128)S(1)} %get-tuple-element.149.mine), channel_id=1, source_target_pairs={{80,112},{81,113},{82,114},{83,115},{84,116},{85,117},{86,118},{87... | collective-permute-start | bytes 786440 | tf_op jit(solution)/shard_map/far13/ppermute | solution.py:363
  289.3 16.6 %collective-permute-start.40 = (f32[512,128]{1,0:T(8,128)S(1)}, f32[512,128]{1,0:T(8,128)S(1)}, u32[]{:S(2)}, u32[]{:S(2)}) collective-permute-start(f32[512,128]{1,0:T(8,128)S(1)} %get-tuple-element.153.mine), channel_id=1, source_target_pairs={{96,112},{97,113},{98,114},{99,115},{100,116},{101,117},{102,118},... | collective-permute-start | bytes 786440 | tf_op jit(solution)/shard_map/near14/ppermute | solution.py:359
  (2 other events, 5.0 us)
Sparse Core Ops, SparseCore 0:
  27.1 58.7 all-gather.5
  87.6 92.2 all-gather.3
where the time goes:
time: 322 us; the launch traced here: 316 us
  waiting for transfers between devices  160 us (50%)
  Pallas kernels  69.6 us (22%)
  starting transfers between devices  56.1 us (17%)
  between operations  14.3 us (4%)
  local copies, waits for them, and re-layouts  14.2 us (4%)
    ppermute x13, waiting for transfers between devices, on_device(): XA = lax.ppermute(mine, 'row', A) if A else zero  64.5 us
    all_gather x1, waiting for transfers between devices, on_device(): g0 = lax.all_gather(u0, 'col', axis=0, tiled=False).reshape(2, R, half, nb)  37 us
    ppermute x14, waiting for transfers between devices, on_device(): XB = lax.ppermute(mine, 'row', B) if B else zero  29.1 us
    pallas_call x15, Pallas kernels, near_call(): pl.pallas_call(kernel, out_shape=tuple(outs), in_specs=[sspec(), sspec()]...  27.6 us
    pallas_call x13, Pallas kernels, far_call(): pl.pallas_call(kernel, out_shape=tuple(outs), in_specs=[sspec(), sspec()]...  25.8 us
    ppermute x14, starting transfers between devices, on_device(): XB = lax.ppermute(mine, 'row', B) if B else zero  15.9 us
    ppermute x13, starting transfers between devices, on_device(): XA = lax.ppermute(mine, 'row', A) if A else zero  15 us
    ppermute x15, starting transfers between devices, on_device(): P1 = lax.ppermute(mine, 'row', [(s, (s + 1) % R)])  12.7 us
  transfers between devices with their start and end apart: 46, of which 16 were waited for; matrix products, arithmetic and copies ran while one was open for 1% of the time, Pallas kernels for 21%

commit v1 on v0

--- a/solution.py
+++ b/solution.py
@@ -132,12 +132,12 @@
     )(g)
 
 
-def prep_call(tab, base, hi, lo, acc):
+def prep_call(row, hi, lo, acc):
     nb, width = acc.shape
 
-    def kernel(tab, hi, lo, acc, nearh, nearl, cur):
-        ki = tab[base]
-        kn = tab[base + 1]
+    def kernel(row, hi, lo, acc, nearh, nearl, cur):
+        ki = nth(row, 0)
+        kn = nth(row, 1)
         w = jnp.concatenate([hi[kn], lo[kn]], 1)
         a = wide(acc[...])
 
@@ -151,25 +151,25 @@
     return pl.pallas_call(
         kernel,
         out_shape=(sq, sq, jax.ShapeDtypeStruct((nb, width), F32)),
-        in_specs=[sspec()] + [vspec()] * 3,
+        in_specs=[vspec()] + [vspec()] * 3,
         out_specs=(vspec(),) * 3,
         compiler_params=params(8),
         name="prep",
-    )(tab, hi, lo, acc)
-
-
-ROW = 8
-
-
-def near_call(tab, tok, nearh, nearl, got, cur, mine, store):
+    )(row, hi, lo, acc)
+
+
+def nth(row, n):
+    return jnp.max(row[n : n + 1, :])
+
+
+def near_call(row, nearh, nearl, got, cur, mine, store):
     keep = store is not None
 
-    def kernel(tab, tok, nearh, nearl, got, cur, mine, *rest):
-        out, tok_out = rest[-2:]
-        at = tok[0] * ROW
-        tok_out[0] = tok[0] + 1
-
-        @pl.when(tab[at + 6] > 0)
+    def kernel(row, nearh, nearl, got, cur, mine, *rest):
+        out = rest[-1]
+        turn = nth(row, 6)
+
+        @pl.when(turn > 0)
         def _():
             w = wide(got[...])
 
@@ -178,46 +178,43 @@
 
             rows_loop(out.shape[0], mul)
             if keep:
-                k = tab[at + 7]
+                k = nth(row, 7)
                 rest[1][k] = got[...]
                 rest[1][k + 1] = out[...]
 
-        @pl.when(tab[at + 6] == 0)
+        @pl.when(turn == 0)
         def _():
             out[...] = mine[...]
 
-    outs = [jax.ShapeDtypeStruct(mine.shape, F32), jax.ShapeDtypeStruct((1,), jnp.int32)]
-    ospecs = [vspec(), sspec()]
-    args = [tab, tok, nearh, nearl, got, cur, mine]
+    outs = [jax.ShapeDtypeStruct(mine.shape, F32)]
+    args = [row, nearh, nearl, got, cur, mine]
     if keep:
         outs.insert(0, jax.ShapeDtypeStruct(store.shape, F32))
-        ospecs.insert(0, vspec())
         args.append(store)
     res = pl.pallas_call(
         kernel,
         out_shape=tuple(outs),
-        in_specs=[sspec(), sspec()] + [vspec()] * (len(args) - 2),
-        out_specs=tuple(ospecs),
-        input_output_aliases={7: 0} if keep else {},
+        in_specs=[vspec()] * len(args),
+        out_specs=(vspec(),) * len(outs),
+        input_output_aliases={6: 0} if keep else {},
         compiler_params=params(4),
         name="near",
     )(*args)
     return res if keep else (None,) + tuple(res)
 
 
-def far_call(tab, tok, hi, lo, acc, cur, xb, xa, store):
+def far_call(row, done, hi, lo, acc, cur, xb, xa, store):
     nb = acc.shape[0]
     keep = store is not None
 
-    def kernel(tab, tok, hi, lo, acc, cur, xb, xa, *rest):
+    def kernel(row, done, hi, lo, acc, cur, xb, xa, *rest):
         acc_out, cur_out = rest[-2:]
-        at = (tok[0] - 1) * ROW
-
-        @pl.when(tab[at + 2] > 0)
+
+        @pl.when(nth(row, 2) > 0)
         def _():
-            kb = tab[at + 0]
-            ka = tab[at + 1]
-            ki = tab[at + 5]
+            kb = nth(row, 0)
+            ka = nth(row, 1)
+            ki = nth(row, 5)
             wb = wide(xb[...])
             wa = wide(xa[...])
 
@@ -232,12 +229,12 @@
 
             rows_loop(nb, mul2)
             if keep:
-                rest[1][tab[at + 3]] = xb[...]
-                rest[1][tab[at + 4]] = xa[...]
+                rest[1][nth(row, 3)] = xb[...]
+                rest[1][nth(row, 4)] = xa[...]
 
     out = jax.ShapeDtypeStruct(acc.shape, F32)
     outs = [out, out]
-    args = [tab, tok, hi, lo, acc, cur, xb, xa]
+    args = [row, done, hi, lo, acc, cur, xb, xa]
     alias = {4: 0, 5: 1}
     if keep:
         outs.insert(0, jax.ShapeDtypeStruct(store.shape, F32))
@@ -246,7 +243,7 @@
     res = pl.pallas_call(
         kernel,
         out_shape=tuple(outs),
-        in_specs=[sspec(), sspec()] + [vspec()] * (len(args) - 2),
+        in_specs=[vspec(), aspec()] + [vspec()] * (len(args) - 2),
         out_specs=(vspec(),) * len(outs),
         input_output_aliases=alias,
         compiler_params=params(4),
@@ -255,20 +252,20 @@
     return res if keep else (None,) + tuple(res)
 
 
-def bulk_call(tab, row, hi, lo, store, acc, xb, xa, count):
+def bulk_call(row, hi, lo, store, acc, xb, xa, count):
     nb, width = acc.shape
 
-    def kernel(tab, hi, lo, store, acc, xb, xa, out, last):
+    def kernel(row, hi, lo, store, acc, xb, xa, out, last):
         out[...] = acc[...]
 
         def one(k, _):
             last[...] = store[k]
 
-            @pl.when((tab[row * ROW + 2] > 0) & (tab[row * ROW + 3] == k))
+            @pl.when((nth(row, 2) > 0) & (nth(row, 3) == k))
             def _():
                 last[...] = xb[...]
 
-            @pl.when((tab[row * ROW + 2] > 0) & (tab[row * ROW + 4] == k))
+            @pl.when((nth(row, 2) > 0) & (nth(row, 4) == k))
             def _():
                 last[...] = xa[...]
 
@@ -285,12 +282,12 @@
     return pl.pallas_call(
         kernel,
         out_shape=jax.ShapeDtypeStruct(acc.shape, F32),
-        in_specs=[sspec()] + [vspec()] * 6,
+        in_specs=[vspec()] + [vspec()] * 6,
         out_specs=vspec(),
         scratch_shapes=[VMEM((nb, width), F32)],
         compiler_params=params(4),
         name="bulk",
-    )(tab, hi, lo, store, acc, xb, xa)
+    )(row, hi, lo, store, acc, xb, xa)
 
 
 def after(x, *others):
@@ -326,6 +323,10 @@
     state = got.reshape(C, blocks, sub, width).transpose(1, 0, 2, 3).reshape(blocks, nb, width)
     acc, acc1 = state[0], state[1]
 
+    def sublanes(*v):
+        v = v + (0,) * (8 - len(v))
+        return jnp.broadcast_to(ints(*v)[:, None], (8, 128))
+
     rows = []
     for t in range(C - 1):
         q = (p - t) % R
@@ -335,7 +336,7 @@
         inwin = (q >= 2) & (q <= 4)
         first = t + 1 < R
         top_k = R - 1 if first else C - 1
-        rows += [
+        rows.append(sublanes(
             jnp.clip(kB, 0, top_k),
             jnp.clip(kA, 0, top_k),
             inwin,
@@ -344,15 +345,16 @@
             p if first else R + p,
             p == (t + 1) % R,
             min(t, R - 1),
-        ]
-    tab = ints(*rows, p, jnp.maximum(p - 1, 0), R + p, R + p - 1)
+        ))
+    rows += [sublanes(p, jnp.maximum(p - 1, 0)), sublanes(R + p, R + p - 1)]
     hi, lo = load_call(g0)
-    nearh, nearl, cur = prep_call(tab, (C - 1) * ROW, hi, lo, acc)
+    rows = lax.optimization_barrier(tuple(rows) + (acc,))
+    acc = rows[-1]
+    nearh, nearl, cur = prep_call(rows[C - 1], hi, lo, acc)
     zero = jnp.zeros((nb, width), F32)
     mine = jnp.where(p == 0, cur, zero)
     store = jnp.zeros((R + 1, nb, width), F32)
     store = lax.dynamic_update_index_in_dim(store, mine, 0, 0)
-    tok = jnp.zeros((1,), jnp.int32)
     for t in range(C - 1):
         s = t % R
         with jax.named_scope(f"near{t}"):
@@ -363,15 +365,15 @@
             XB = lax.ppermute(mine, "row", B) if B else zero
             XA = lax.ppermute(mine, "row", A) if A else zero
         first = t + 1 < R
-        store, mine, tok = near_call(tab, tok, nearh, nearl, P1, cur, mine, store if first else None)
+        store, mine = near_call(rows[t], nearh, nearl, P1, cur, mine, store if first else None)
         if first:
             out0 = mine
         if t + 1 == R - 1:
             hi, lo = load_call(g1)
-            acc = bulk_call(tab, t, hi, lo, store, acc1, XB, XA, R)
-            nearh, nearl, cur = prep_call(tab, (C - 1) * ROW + 2, hi, lo, acc)
+            acc = bulk_call(rows[t], hi, lo, store, acc1, XB, XA, R)
+            nearh, nearl, cur = prep_call(rows[C], hi, lo, acc)
         elif B or A:
-            store, acc, cur = far_call(tab, tok, hi, lo, acc, cur, XB, XA, store if first else None)
+            store, acc, cur = far_call(rows[t], mine, hi, lo, acc, cur, XB, XA, store if first else None)
     return jnp.concatenate([out0, mine], 0)
 
 

time: 322 us -> 311 us (0.966); the launches traced: 316 us -> 310 us
  Pallas kernels: 69.6 us -> 39.6 us
  waiting for transfers between devices: 160 us -> 175 us
  starting transfers between devices: 56.1 us -> 62.8 us
    pallas_call x28, Pallas kernels: 53.4 us -> 20.7 us  [the longest x13 15 us: far_call(): pl.pallas_call(kernel, out_shape=tuple(outs), in_specs=[vspec(), aspec()]...]
    ppermute x13, waiting for transfers between devices: 64.5 us -> 81.6 us  [on_device(): XA = lax.ppermute(mine, 'row', A) if A else zero]
    ppermute x13, starting transfers between devices: 15 us -> 21.2 us  [on_device(): XA = lax.ppermute(mine, 'row', A) if A else zero]
    pallas_call x1, Pallas kernels: 5.95 us -> 9.41 us  [bulk_call(): pl.pallas_call(kernel, out_shape=jax.ShapeDtypeStruct(acc.shape, F32), in...]
  transfers between devices with their start and end apart: 46 -> 46, of which waited for: 16 -> 19; matrix products, arithmetic and copies ran while one was open for 1% -> 2% of each run, Pallas kernels for 21% -> 12%
where the time goes in v1:
time: 311 us; the launch traced here: 310 us
  waiting for transfers between devices  175 us (56%)
  starting transfers between devices  62.8 us (20%)
  Pallas kernels  39.6 us (13%)
  local copies, waits for them, and re-layouts  16.4 us (5%)
  between operations  14.3 us (5%)
    ppermute x13, waiting for transfers between devices, on_device(): XA = lax.ppermute(mine, 'row', A) if A else zero  81.6 us
    all_gather x1, waiting for transfers between devices, on_device(): g0 = lax.all_gather(u0, 'col', axis=0, tiled=False).reshape(2, R, half, nb)  35.9 us
    ppermute x14, waiting for transfers between devices, on_device(): XB = lax.ppermute(mine, 'row', B) if B else zero  29 us
    ppermute x13, starting transfers between devices, on_device(): XA = lax.ppermute(mine, 'row', A) if A else zero  21.2 us
    ppermute x14, starting transfers between devices, on_device(): XB = lax.ppermute(mine, 'row', B) if B else zero  16.5 us
    pallas_call x13, Pallas kernels, far_call(): pl.pallas_call(kernel, out_shape=tuple(outs), in_specs=[vspec(), aspec()]...  15 us
    ppermute x15, starting transfers between devices, on_device(): P1 = lax.ppermute(mine, 'row', [(s, (s + 1) % R)])  12.7 us
    ppermute x1, waiting for transfers between devices, on_device(): moved = lax.ppermute(top[half:], 'col', [(i, i + R) for i in range(R)])  11.4 us
  transfers between devices with their start and end apart: 46, of which 19 were waited for; matrix products, arithmetic and copies ran while one was open for 2% of the time, Pallas kernels for 12%

profile of v1, /device:TPU:120, one launch (start us, length us, event | category | flops | bytes accessed | tf_op | source)
XLA Modules:
  0.0 309.8 jit_solution(7028508499174183448)
XLA Ops:
  6.6 1.6 copy-done.2
  9.7 4.9 %collective-permute-start = (f32[256,512]{1,0:T(8,128)}, f32[256,512]{1,0:T(8,128)S(1)}, u32[]{:S(2)}, u32[]{:S(2)}) collective-permute-start(f32[256,512]{1,0:T(8,128)} %slice_bitcast_fusion), channel_id=1, source_target_pairs={{0,8},{1,9},{2,10},{3,11},{4,12},{5,13},{6,14},{7,15},{16,24},{17,... | collective-permute-start | bytes 1572872 | tf_op jit(solution)/shard_map/ppermute | solution.py:315
  14.7 11.4 %collective-permute-done = f32[256,512]{1,0:T(8,128)S(1)} collective-permute-done((f32[256,512]{1,0:T(8,128)}, f32[256,512]{1,0:T(8,128)S(1)}, u32[]{:S(2)}, u32[]{:S(2)}) %collective-permute-start) | collective-permute-done | bytes 524320 | tf_op jit(solution)/shard_map/ppermute | solution.py:315
  29.2 7.4 %all-to-all-start = ((f32[16,64,128]{2,1,0:T(8,128)}), f32[16,64,128]{2,1,0:T(8,128)S(1)}, u32[]{:S(2)}, u32[]{:S(2)}) async-start(f32[16,64,128]{2,1,0:T(8,128)} %copy.43), calls=%async_computation | async-start | bytes 1048576 | tf_op jit(solution)/shard_map/all_to_all | solution.py:322
  38.0 10.8 %all-to-all-done = f32[16,64,128]{2,1,0:T(8,128)S(1)} async-done(((f32[16,64,128]{2,1,0:T(8,128)}), f32[16,64,128]{2,1,0:T(8,128)S(1)}, u32[]{:S(2)}, u32[]{:S(2)}) %all-to-all-start) | async-done | bytes 524320 | tf_op jit(solution)/shard_map/all_to_all | solution.py:322
  50.0 35.9 %all-gather.6.cloned.1.call-done = f32[4096,512]{1,0:T(8,128)} async-done(((f32[256,512]{1,0:T(8,128)}), f32[4096,512]{1,0:T(8,128)}) %all-gather.6.cloned.1.call-update) | async-done | bytes 8388624 | tf_op jit(solution)/shard_map/all_gather | solution.py:318
  85.9 3.4 %copy-done.1 = f32[4096,512]{1,0:T(8,128)S(1)} copy-done((f32[4096,512]{1,0:T(8,128)S(1)}, f32[4096,512]{1,0:T(8,128)}, u32[]{:S(2)}) %copy-start.1) | copy-done | bytes 8388632
  89.3 2.0 load.2
  91.3 2.1 prep.2
  100.9 1.3 collective-permute-start.12
  102.2 1.3 collective-permute-start.11
  104.7 1.3 collective-permute-start.15
  106.0 1.3 collective-permute-start.14
  107.3 38.0 %collective-permute-done.12.xa = f32[512,128]{1,0:T(8,128)S(1)} collective-permute-done((f32[512,128]{1,0:T(8,128)S(1)}, f32[512,128]{1,0:T(8,128)S(1)}, u32[]{:S(2)}, u32[]{:S(2)}) %collective-permute-start.12) | collective-permute-done | bytes 262176 | tf_op jit(solution)/shard_map/far3/ppermute | solution.py:366
  145.3 2.2 far.16
  148.4 1.3 collective-permute-start.18
  149.7 1.3 collective-permute-start.17
  151.0 16.8 %collective-permute-done.15.xa = f32[512,128]{1,0:T(8,128)S(1)} collective-permute-done((f32[512,128]{1,0:T(8,128)S(1)}, f32[512,128]{1,0:T(8,128)S(1)}, u32[]{:S(2)}, u32[]{:S(2)}) %collective-permute-start.15) | collective-permute-done | bytes 262176 | tf_op jit(solution)/shard_map/far4/ppermute | solution.py:366
  167.9 4.9 %collective-permute-done.14.xb = f32[512,128]{1,0:T(8,128)S(1)} collective-permute-done((f32[512,128]{1,0:T(8,128)S(1)}, f32[512,128]{1,0:T(8,128)S(1)}, u32[]{:S(2)}, u32[]{:S(2)}) %collective-permute-start.14) | collective-permute-done | bytes 262176 | tf_op jit(solution)/shard_map/far4/ppermute | solution.py:365
  172.7 2.2 far.17
  177.2 1.4 collective-permute-start.19
  178.6 9.5 %collective-permute-done.18.xa = f32[512,128]{1,0:T(8,128)S(1)} collective-permute-done((f32[512,128]{1,0:T(8,128)S(1)}, f32[512,128]{1,0:T(8,128)S(1)}, u32[]{:S(2)}, u32[]{:S(2)}) %collective-permute-start.18) | collective-permute-done | bytes 262176 | tf_op jit(solution)/shard_map/far5/ppermute | solution.py:366
  188.0 2.4 far.18
  190.4 2.7 collective-permute-done.16.got
  194.2 2.0 collective-permute-start.21
  196.2 1.4 collective-permute-start.24
  197.6 2.0 collective-permute-start.23
  199.6 5.8 %copy-done = f32[16,512,512]{2,1,0:T(8,128)S(1)} copy-done((f32[16,512,512]{2,1,0:T(8,128)S(1)}, f32[16,512,512]{2,1,0:T(8,128)}, u32[]{:S(2)}) %copy-start) | copy-done | bytes 16777240
  205.3 2.8 load.3
  208.1 9.4 %bulk.1.acc = f32[512,128]{1,0:T(8,128)S(1)} custom-call(s32[8,128]{1,0:T(8,128)S(1)} %broadcast_in_dim.45.row, bf16[16,512,512]{2,1,0:T(8,128)(2,1)S(1)} %get-tuple-element.123.hi, bf16[16,512,512]{2,1,0:T(8,128)(2,1)S(1)} %get-tuple-element.124.lo, f32[9,512,128]{2,1,0:T(8,128)S(1)} %get-tuple-element.125.store, f32[512,128]{1,0:T(8,128)S(1)} %bitcast.114, ...), custom_call_target="tpu_custom_call" | custom-call | tf_op jit(solution)/shard_map/bulk/pallas_call | solution.py:282
  217.6 2.1 prep.3
  221.5 5.8 %collective-permute-start.27 = (f32[512,128]{1,0:T(8,128)S(1)}, f32[512,128]{1,0:T(8,128)S(1)}, u32[]{:S(2)}, u32[]{:S(2)}) collective-permute-start(f32[512,128]{1,0:T(8,128)S(1)} %near.22.done.mine), channel_id=1, source_target_pairs={{112,32},{96,48},{80,64},{113,33},{97,49},{81,65},{114,34},{98,50}... | collective-permute-start | bytes 786440 | tf_op jit(solution)/shard_map/far8/ppermute | solution.py:366
  227.3 1.3 collective-permute-start.26
  230.8 1.3 collective-permute-start.30
  232.1 1.3 collective-permute-start.29
  233.9 12.4 %collective-permute-done.26.xb = f32[512,128]{1,0:T(8,128)S(1)} collective-permute-done((f32[512,128]{1,0:T(8,128)S(1)}, f32[512,128]{1,0:T(8,128)S(1)}, u32[]{:S(2)}, u32[]{:S(2)}) %collective-permute-start.26) | collective-permute-done | bytes 262176 | tf_op jit(solution)/shard_map/far8/ppermute | solution.py:365
  247.5 3.0 collective-permute-start.33
  257.4 1.3 collective-permute-start.39
  258.7 1.3 collective-permute-start.38
  260.0 5.9 %collective-permute-done.36.xa = f32[512,128]{1,0:T(8,128)S(1)} collective-permute-done((f32[512,128]{1,0:T(8,128)S(1)}, f32[512,128]{1,0:T(8,128)S(1)}, u32[]{:S(2)}, u32[]{:S(2)}) %collective-permute-start.36) | collective-permute-done | bytes 262176 | tf_op jit(solution)/shard_map/far11/ppermute | solution.py:366
  265.9 5.5 %collective-permute-done.35.xb = f32[512,128]{1,0:T(8,128)S(1)} collective-permute-done((f32[512,128]{1,0:T(8,128)S(1)}, f32[512,128]{1,0:T(8,128)S(1)}, u32[]{:S(2)}, u32[]{:S(2)}) %collective-permute-start.35) | collective-permute-done | bytes 262176 | tf_op jit(solution)/shard_map/far11/ppermute | solution.py:365
  271.4 1.9 far.23
  276.9 5.5 %collective-permute-done.39.xa = f32[512,128]{1,0:T(8,128)S(1)} collective-permute-done((f32[512,128]{1,0:T(8,128)S(1)}, f32[512,128]{1,0:T(8,128)S(1)}, u32[]{:S(2)}, u32[]{:S(2)}) %collective-permute-start.39) | collective-permute-done | bytes 262176 | tf_op jit(solution)/shard_map/far12/ppermute | solution.py:366
  283.0 1.9 far.24
  286.5 4.2 %collective-permute-done.42.xa = f32[512,128]{1,0:T(8,128)S(1)} collective-permute-done((f32[512,128]{1,0:T(8,128)S(1)}, f32[512,128]{1,0:T(8,128)S(1)}, u32[]{:S(2)}, u32[]{:S(2)}) %collective-permute-start.42) | collective-permute-done | bytes 262176 | tf_op jit(solution)/shard_map/far13/ppermute | solution.py:366
  290.6 5.4 %collective-permute-done.41.xb = f32[512,128]{1,0:T(8,128)S(1)} collective-permute-done((f32[512,128]{1,0:T(8,128)S(1)}, f32[512,128]{1,0:T(8,128)S(1)}, u32[]{:S(2)}, u32[]{:S(2)}) %collective-permute-start.41) | collective-permute-done | bytes 262176 | tf_op jit(solution)/shard_map/far13/ppermute | solution.py:365
  296.0 1.9 far.25
  298.0 3.3 %collective-permute-done.40.got = f32[512,128]{1,0:T(8,128)S(1)} collective-permute-done((f32[512,128]{1,0:T(8,128)S(1)}, f32[512,128]{1,0:T(8,128)S(1)}, u32[]{:S(2)}, u32[]{:S(2)}) %collective-permute-start.40) | collective-permute-done | bytes 262176 | tf_op jit(solution)/shard_map/near14/ppermute | solution.py:361
  (135 shorter events, 39.6 us)
Async XLA Ops:
  6.5 79.4 %all-gather.6.cloned.1.call-start = ((), (), s32[]{:S(2)}) async-start(), calls=%async_computation.2 | async-start | bytes 8912896 | tf_op jit(solution)/shard_map/all_gather | solution.py:318
  9.7 16.4 %collective-permute-start = (f32[256,512]{1,0:T(8,128)}, f32[256,512]{1,0:T(8,128)S(1)}, u32[]{:S(2)}, u32[]{:S(2)}) collective-permute-start(f32[256,512]{1,0:T(8,128)} %slice_bitcast_fusion), channel_id=1, source_target_pairs={{0,8},{1,9},{2,10},{3,11},{4,12},{5,13},{6,14},{7,15},{16,24},{17,... | collective-permute-start | bytes 1572872 | tf_op jit(solution)/shard_map/ppermute | solution.py:315
  14.7 13.5 %copy-start.3 = (f32[64,2048]{1,0:T(8,128)S(1)}, f32[64,2048]{1,0:T(8,128)}, u32[]{:S(2)}) copy-start(f32[64,2048]{1,0:T(8,128)} %param.3) | copy-start | bytes 1572868
  27.0 172.6 %all-gather.4.cloned.1.call-start = ((), (), s32[]{:S(2)}) async-start(), calls=%async_computation.1 | async-start | bytes 17825792 | tf_op jit(solution)/shard_map/all_gather | solution.py:319
  29.2 19.6 %all-to-all-start = ((f32[16,64,128]{2,1,0:T(8,128)}), f32[16,64,128]{2,1,0:T(8,128)S(1)}, u32[]{:S(2)}, u32[]{:S(2)}) async-start(f32[16,64,128]{2,1,0:T(8,128)} %copy.43), calls=%async_computation | async-start | bytes 1048576 | tf_op jit(solution)/shard_map/all_to_all | solution.py:322
  93.3 1.6 collective-permute-start.1
  94.0 3.2 %collective-permute-start.3 = (f32[512,128]{1,0:T(8,128)S(1)}, f32[512,128]{1,0:T(8,128)S(1)}, u32[]{:S(2)}, u32[]{:S(2)}) collective-permute-start(f32[512,128]{1,0:T(8,128)S(1)} %broadcast_select_fusion.mine), channel_id=1, source_target_pairs={{0,32},{1,33},{2,34},{3,35},{4,36},{5,37},{6,38},{7,39},{8,40},{9,... | collective-permute-start | bytes 786440 | tf_op jit(solution)/shard_map/far0/ppermute | solution.py:365
  95.2 2.3 collective-permute-start.2
  95.9 3.9 %collective-permute-start.6 = (f32[512,128]{1,0:T(8,128)S(1)}, f32[512,128]{1,0:T(8,128)S(1)}, u32[]{:S(2)}, u32[]{:S(2)}) collective-permute-start(f32[512,128]{1,0:T(8,128)S(1)} %get-tuple-element.91.done.mine), channel_id=1, source_target_pairs={{0,48},{1,49},{2,50},{3,51},{4,52},{5,53},{6,54},{7,55},{8,56},{9,... | collective-permute-start | bytes 786440 | tf_op jit(solution)/shard_map/far1/ppermute | solution.py:366
  96.5 3.2 %collective-permute-start.5 = (f32[512,128]{1,0:T(8,128)S(1)}, f32[512,128]{1,0:T(8,128)S(1)}, u32[]{:S(2)}, u32[]{:S(2)}) collective-permute-start(f32[512,128]{1,0:T(8,128)S(1)} %get-tuple-element.91.done.mine), channel_id=1, source_target_pairs={{16,48},{0,64},{17,49},{1,65},{18,50},{2,66},{19,51},{3,67},{20,52... | collective-permute-start | bytes 786440 | tf_op jit(solution)/shard_map/far1/ppermute | solution.py:365
  97.7 2.3 collective-permute-start.4
  98.4 5.1 %collective-permute-start.9 = (f32[512,128]{1,0:T(8,128)S(1)}, f32[512,128]{1,0:T(8,128)S(1)}, u32[]{:S(2)}, u32[]{:S(2)}) collective-permute-start(f32[512,128]{1,0:T(8,128)S(1)} %get-tuple-element.95.done.mine), channel_id=1, source_target_pairs={{16,64},{0,80},{17,65},{1,81},{18,66},{2,82},{19,67},{3,83},{20,68... | collective-permute-start | bytes 786440 | tf_op jit(solution)/shard_map/far2/ppermute | solution.py:366
  99.1 4.5 %collective-permute-start.8 = (f32[512,128]{1,0:T(8,128)S(1)}, f32[512,128]{1,0:T(8,128)S(1)}, u32[]{:S(2)}, u32[]{:S(2)}) collective-permute-start(f32[512,128]{1,0:T(8,128)S(1)} %get-tuple-element.95.done.mine), channel_id=1, source_target_pairs={{32,64},{16,80},{0,96},{33,65},{17,81},{1,97},{34,66},{18,82},{2,9... | collective-permute-start | bytes 786440 | tf_op jit(solution)/shard_map/far2/ppermute | solution.py:365
  100.3 3.5 %collective-permute-start.7 = (f32[512,128]{1,0:T(8,128)S(1)}, f32[512,128]{1,0:T(8,128)S(1)}, u32[]{:S(2)}, u32[]{:S(2)}) collective-permute-start(f32[512,128]{1,0:T(8,128)S(1)} %get-tuple-element.100.done.mine), channel_id=1, source_target_pairs={{48,64},{49,65},{50,66},{51,67},{52,68},{53,69},{54,70},{55,71},{5... | collective-permute-start | bytes 786440 | tf_op jit(solution)/shard_map/near3/ppermute | solution.py:361
  100.9 44.4 %collective-permute-start.12 = (f32[512,128]{1,0:T(8,128)S(1)}, f32[512,128]{1,0:T(8,128)S(1)}, u32[]{:S(2)}, u32[]{:S(2)}) collective-permute-start(f32[512,128]{1,0:T(8,128)S(1)} %get-tuple-element.100.done.mine), channel_id=1, source_target_pairs={{32,80},{16,96},{0,112},{33,81},{17,97},{1,113},{34,82},{18,98},{2... | collective-permute-start | bytes 786440 | tf_op jit(solution)/shard_map/far3/ppermute | solution.py:366
  102.2 43.1 %collective-permute-start.11 = (f32[512,128]{1,0:T(8,128)S(1)}, f32[512,128]{1,0:T(8,128)S(1)}, u32[]{:S(2)}, u32[]{:S(2)}) collective-permute-start(f32[512,128]{1,0:T(8,128)S(1)} %get-tuple-element.100.done.mine), channel_id=1, source_target_pairs={{48,80},{32,96},{16,112},{49,81},{33,97},{17,113},{50,82},{34,98},... | collective-permute-start | bytes 786440 | tf_op jit(solution)/shard_map/far3/ppermute | solution.py:365
  104.0 43.5 %collective-permute-start.10 = (f32[512,128]{1,0:T(8,128)S(1)}, f32[512,128]{1,0:T(8,128)S(1)}, u32[]{:S(2)}, u32[]{:S(2)}) collective-permute-start(f32[512,128]{1,0:T(8,128)S(1)} %get-tuple-element.105.done.mine), channel_id=1, source_target_pairs={{64,80},{65,81},{66,82},{67,83},{68,84},{69,85},{70,86},{71,87},{7... | collective-permute-start | bytes 786440 | tf_op jit(solution)/shard_map/near4/ppermute | solution.py:361
  104.7 63.2 %collective-permute-start.15 = (f32[512,128]{1,0:T(8,128)S(1)}, f32[512,128]{1,0:T(8,128)S(1)}, u32[]{:S(2)}, u32[]{:S(2)}) collective-permute-start(f32[512,128]{1,0:T(8,128)S(1)} %get-tuple-element.105.done.mine), channel_id=1, source_target_pairs={{48,96},{32,112},{16,0},{49,97},{33,113},{17,1},{50,98},{34,114},{... | collective-permute-start | bytes 786440 | tf_op jit(solution)/shard_map/far4/ppermute | solution.py:366
  106.0 66.7 %collective-permute-start.14 = (f32[512,128]{1,0:T(8,128)S(1)}, f32[512,128]{1,0:T(8,128)S(1)}, u32[]{:S(2)}, u32[]{:S(2)}) collective-permute-start(f32[512,128]{1,0:T(8,128)S(1)} %get-tuple-element.105.done.mine), channel_id=1, source_target_pairs={{64,96},{48,112},{32,0},{65,97},{49,113},{33,1},{66,98},{50,114},{... | collective-permute-start | bytes 786440 | tf_op jit(solution)/shard_map/far4/ppermute | solution.py:365
  147.8 27.2 %collective-permute-start.13 = (f32[512,128]{1,0:T(8,128)S(1)}, f32[512,128]{1,0:T(8,128)S(1)}, u32[]{:S(2)}, u32[]{:S(2)}) collective-permute-start(f32[512,128]{1,0:T(8,128)S(1)} %get-tuple-element.110.done.mine), channel_id=1, source_target_pairs={{80,96},{81,97},{82,98},{83,99},{84,100},{85,101},{86,102},{87,103... | collective-permute-start | bytes 786440 | tf_op jit(solution)/shard_map/near5/ppermute | solution.py:361
  148.4 39.6 %collective-permute-start.18 = (f32[512,128]{1,0:T(8,128)S(1)}, f32[512,128]{1,0:T(8,128)S(1)}, u32[]{:S(2)}, u32[]{:S(2)}) collective-permute-start(f32[512,128]{1,0:T(8,128)S(1)} %get-tuple-element.110.done.mine), channel_id=1, source_target_pairs={{64,112},{48,0},{32,16},{65,113},{49,1},{33,17},{66,114},{50,2},{3... | collective-permute-start | bytes 786440 | tf_op jit(solution)/shard_map/far5/ppermute | solution.py:366
  149.7 38.3 %collective-permute-start.17 = (f32[512,128]{1,0:T(8,128)S(1)}, f32[512,128]{1,0:T(8,128)S(1)}, u32[]{:S(2)}, u32[]{:S(2)}) collective-permute-start(f32[512,128]{1,0:T(8,128)S(1)} %get-tuple-element.110.done.mine), channel_id=1, source_target_pairs={{80,112},{64,0},{48,16},{81,113},{65,1},{49,17},{82,114},{66,2},{5... | collective-permute-start | bytes 786440 | tf_op jit(solution)/shard_map/far5/ppermute | solution.py:365
  175.2 17.9 %collective-permute-start.16 = (f32[512,128]{1,0:T(8,128)S(1)}, f32[512,128]{1,0:T(8,128)S(1)}, u32[]{:S(2)}, u32[]{:S(2)}) collective-permute-start(f32[512,128]{1,0:T(8,128)S(1)} %get-tuple-element.115.done.mine), channel_id=1, source_target_pairs={{96,112},{97,113},{98,114},{99,115},{100,116},{101,117},{102,118},... | collective-permute-start | bytes 786440 | tf_op jit(solution)/shard_map/near6/ppermute | solution.py:361
  176.5 31.6 %collective-permute-start.20 = (f32[512,128]{1,0:T(8,128)S(1)}, f32[512,128]{1,0:T(8,128)S(1)}, u32[]{:S(2)}, u32[]{:S(2)}) collective-permute-start(f32[512,128]{1,0:T(8,128)S(1)} %get-tuple-element.115.done.mine), channel_id=1, source_target_pairs={{80,0},{64,16},{48,32},{81,1},{65,17},{49,33},{82,2},{66,18},{50,3... | collective-permute-start | bytes 786440 | tf_op jit(solution)/shard_map/far6/ppermute | solution.py:366
  177.2 31.0 %collective-permute-start.19 = (f32[512,128]{1,0:T(8,128)S(1)}, f32[512,128]{1,0:T(8,128)}, u32[]{:S(2)}, u32[]{:S(2)}) collective-permute-start(f32[512,128]{1,0:T(8,128)S(1)} %get-tuple-element.115.done.mine), channel_id=1, source_target_pairs={{96,0},{80,16},{64,32},{97,1},{81,17},{65,33},{98,2},{82,18},{66,3... | collective-permute-start | bytes 786440 | tf_op jit(solution)/shard_map/far6/ppermute | solution.py:365
  194.2 25.4 %collective-permute-start.21 = (f32[512,128]{1,0:T(8,128)S(1)}, f32[512,128]{1,0:T(8,128)}, u32[]{:S(2)}, u32[]{:S(2)}) collective-permute-start(f32[512,128]{1,0:T(8,128)S(1)} %get-tuple-element.120.mine), channel_id=1, source_target_pairs={{112,0},{113,1},{114,2},{115,3},{116,4},{117,5},{118,6},{119,7},{1... | collective-permute-start | bytes 786440 | tf_op jit(solution)/shard_map/near7/ppermute | solution.py:361
  196.2 32.4 %collective-permute-start.24 = (f32[512,128]{1,0:T(8,128)S(1)}, f32[512,128]{1,0:T(8,128)}, u32[]{:S(2)}, u32[]{:S(2)}) collective-permute-start(f32[512,128]{1,0:T(8,128)S(1)} %get-tuple-element.120.mine), channel_id=1, source_target_pairs={{96,16},{80,32},{64,48},{97,17},{81,33},{65,49},{98,18},{82,34},{6... | collective-permute-start | bytes 786440 | tf_op jit(solution)/shard_map/far7/ppermute | solution.py:366
  197.6 31.0 %collective-permute-start.23 = (f32[512,128]{1,0:T(8,128)S(1)}, f32[512,128]{1,0:T(8,128)}, u32[]{:S(2)}, u32[]{:S(2)}) collective-permute-start(f32[512,128]{1,0:T(8,128)S(1)} %get-tuple-element.120.mine), channel_id=1, source_target_pairs={{112,16},{96,32},{80,48},{113,17},{97,33},{81,49},{114,18},{98,34}... | collective-permute-start | bytes 786440 | tf_op jit(solution)/shard_map/far7/ppermute | solution.py:365
  199.6 5.8 %copy-start = (f32[16,512,512]{2,1,0:T(8,128)S(1)}, f32[16,512,512]{2,1,0:T(8,128)}, u32[]{:S(2)}) copy-start(f32[16,512,512]{2,1,0:T(8,128)} %all-gather.4.cloned.1.call-done) | copy-start | bytes 50331652
  220.8 9.1 %collective-permute-start.22 = (f32[512,128]{1,0:T(8,128)S(1)}, f32[512,128]{1,0:T(8,128)S(1)}, u32[]{:S(2)}, u32[]{:S(2)}) collective-permute-start(f32[512,128]{1,0:T(8,128)S(1)} %near.22.done.mine), channel_id=1, source_target_pairs={{0,16},{1,17},{2,18},{3,19},{4,20},{5,21},{6,22},{7,23},{8,24},{9,... | collective-permute-start | bytes 786440 | tf_op jit(solution)/shard_map/near8/ppermute | solution.py:361
  221.5 12.5 %collective-permute-start.27 = (f32[512,128]{1,0:T(8,128)S(1)}, f32[512,128]{1,0:T(8,128)S(1)}, u32[]{:S(2)}, u32[]{:S(2)}) collective-permute-start(f32[512,128]{1,0:T(8,128)S(1)} %near.22.done.mine), channel_id=1, source_target_pairs={{112,32},{96,48},{80,64},{113,33},{97,49},{81,65},{114,34},{98,50}... | collective-permute-start | bytes 786440 | tf_op jit(solution)/shard_map/far8/ppermute | solution.py:366
  227.3 19.1 %collective-permute-start.26 = (f32[512,128]{1,0:T(8,128)S(1)}, f32[512,128]{1,0:T(8,128)S(1)}, u32[]{:S(2)}, u32[]{:S(2)}) collective-permute-start(f32[512,128]{1,0:T(8,128)S(1)} %near.22.done.mine), channel_id=1, source_target_pairs={{0,32},{112,48},{96,64},{1,33},{113,49},{97,65},{2,34},{114,50},{9... | collective-permute-start | bytes 786440 | tf_op jit(solution)/shard_map/far8/ppermute | solution.py:365
  230.1 16.5 %collective-permute-start.25 = (f32[512,128]{1,0:T(8,128)S(1)}, f32[512,128]{1,0:T(8,128)S(1)}, u32[]{:S(2)}, u32[]{:S(2)}) collective-permute-start(f32[512,128]{1,0:T(8,128)S(1)} %near.23.done.mine), channel_id=1, source_target_pairs={{16,32},{17,33},{18,34},{19,35},{20,36},{21,37},{22,38},{23,39},{2... | collective-permute-start | bytes 786440 | tf_op jit(solution)/shard_map/near9/ppermute | solution.py:361
  230.8 20.4 %collective-permute-start.30 = (f32[512,128]{1,0:T(8,128)S(1)}, f32[512,128]{1,0:T(8,128)S(1)}, u32[]{:S(2)}, u32[]{:S(2)}) collective-permute-start(f32[512,128]{1,0:T(8,128)S(1)} %near.23.done.mine), channel_id=1, source_target_pairs={{0,48},{112,64},{96,80},{1,49},{113,65},{97,81},{2,50},{114,66},{9... | collective-permute-start | bytes 786440 | tf_op jit(solution)/shard_map/far9/ppermute | solution.py:366
  232.1 19.3 %collective-permute-start.29 = (f32[512,128]{1,0:T(8,128)S(1)}, f32[512,128]{1,0:T(8,128)S(1)}, u32[]{:S(2)}, u32[]{:S(2)}) collective-permute-start(f32[512,128]{1,0:T(8,128)S(1)} %near.23.done.mine), channel_id=1, source_target_pairs={{16,48},{0,64},{112,80},{17,49},{1,65},{113,81},{18,50},{2,66},{11... | collective-permute-start | bytes 786440 | tf_op jit(solution)/shard_map/far9/ppermute | solution.py:365
  246.8 4.8 %collective-permute-start.28 = (f32[512,128]{1,0:T(8,128)S(1)}, f32[512,128]{1,0:T(8,128)S(1)}, u32[]{:S(2)}, u32[]{:S(2)}) collective-permute-start(f32[512,128]{1,0:T(8,128)S(1)} %near.24.done.mine), channel_id=1, source_target_pairs={{32,48},{33,49},{34,50},{35,51},{36,52},{37,53},{38,54},{39,55},{4... | collective-permute-start | bytes 786440 | tf_op jit(solution)/shard_map/near10/ppermute | solution.py:361
  247.5 8.7 %collective-permute-start.33 = (f32[512,128]{1,0:T(8,128)S(1)}, f32[512,128]{1,0:T(8,128)S(1)}, u32[]{:S(2)}, u32[]{:S(2)}) collective-permute-start(f32[512,128]{1,0:T(8,128)S(1)} %near.24.done.mine), channel_id=1, source_target_pairs={{16,64},{0,80},{112,96},{17,65},{1,81},{113,97},{18,66},{2,82},{11... | collective-permute-start | bytes 786440 | tf_op jit(solution)/shard_map/far10/ppermute | solution.py:366
  250.5 5.7 %collective-permute-start.32 = (f32[512,128]{1,0:T(8,128)S(1)}, f32[512,128]{1,0:T(8,128)S(1)}, u32[]{:S(2)}, u32[]{:S(2)}) collective-permute-start(f32[512,128]{1,0:T(8,128)S(1)} %near.24.done.mine), channel_id=1, source_target_pairs={{32,64},{16,80},{0,96},{33,65},{17,81},{1,97},{34,66},{18,82},{2,9... | collective-permute-start | bytes 786440 | tf_op jit(solution)/shard_map/far10/ppermute | solution.py:365
  251.8 4.6 %collective-permute-start.31 = (f32[512,128]{1,0:T(8,128)S(1)}, f32[512,128]{1,0:T(8,128)S(1)}, u32[]{:S(2)}, u32[]{:S(2)}) collective-permute-start(f32[512,128]{1,0:T(8,128)S(1)} %near.25.done.mine), channel_id=1, source_target_pairs={{48,64},{49,65},{50,66},{51,67},{52,68},{53,69},{54,70},{55,71},{5... | collective-permute-start | bytes 786440 | tf_op jit(solution)/shard_map/near11/ppermute | solution.py:361
  252.5 13.4 %collective-permute-start.36 = (f32[512,128]{1,0:T(8,128)S(1)}, f32[512,128]{1,0:T(8,128)S(1)}, u32[]{:S(2)}, u32[]{:S(2)}) collective-permute-start(f32[512,128]{1,0:T(8,128)S(1)} %near.25.done.mine), channel_id=1, source_target_pairs={{32,80},{16,96},{0,112},{33,81},{17,97},{1,113},{34,82},{18,98},{2... | collective-permute-start | bytes 786440 | tf_op jit(solution)/shard_map/far11/ppermute | solution.py:366
  253.8 17.6 %collective-permute-start.35 = (f32[512,128]{1,0:T(8,128)S(1)}, f32[512,128]{1,0:T(8,128)S(1)}, u32[]{:S(2)}, u32[]{:S(2)}) collective-permute-start(f32[512,128]{1,0:T(8,128)S(1)} %near.25.done.mine), channel_id=1, source_target_pairs={{48,80},{32,96},{16,112},{49,81},{33,97},{17,113},{50,82},{34,98},... | collective-permute-start | bytes 786440 | tf_op jit(solution)/shard_map/far11/ppermute | solution.py:365
  256.7 16.7 %collective-permute-start.34 = (f32[512,128]{1,0:T(8,128)S(1)}, f32[512,128]{1,0:T(8,128)S(1)}, u32[]{:S(2)}, u32[]{:S(2)}) collective-permute-start(f32[512,128]{1,0:T(8,128)S(1)} %near.26.done.mine), channel_id=1, source_target_pairs={{64,80},{65,81},{66,82},{67,83},{68,84},{69,85},{70,86},{71,87},{7... | collective-permute-start | bytes 786440 | tf_op jit(solution)/shard_map/near12/ppermute | solution.py:361
  257.4 25.1 %collective-permute-start.39 = (f32[512,128]{1,0:T(8,128)S(1)}, f32[512,128]{1,0:T(8,128)S(1)}, u32[]{:S(2)}, u32[]{:S(2)}) collective-permute-start(f32[512,128]{1,0:T(8,128)S(1)} %near.26.done.mine), channel_id=1, source_target_pairs={{48,96},{32,112},{49,97},{33,113},{50,98},{34,114},{51,99},{35,115... | collective-permute-start | bytes 786440 | tf_op jit(solution)/shard_map/far12/ppermute | solution.py:366
  258.7 24.3 %collective-permute-start.38 = (f32[512,128]{1,0:T(8,128)S(1)}, f32[512,128]{1,0:T(8,128)S(1)}, u32[]{:S(2)}, u32[]{:S(2)}) collective-permute-start(f32[512,128]{1,0:T(8,128)S(1)} %near.26.done.mine), channel_id=1, source_target_pairs={{64,96},{48,112},{65,97},{49,113},{66,98},{50,114},{67,99},{51,115... | collective-permute-start | bytes 786440 | tf_op jit(solution)/shard_map/far12/ppermute | solution.py:365
  273.6 11.3 %collective-permute-start.37 = (f32[512,128]{1,0:T(8,128)S(1)}, f32[512,128]{1,0:T(8,128)S(1)}, u32[]{:S(2)}, u32[]{:S(2)}) collective-permute-start(f32[512,128]{1,0:T(8,128)S(1)} %near.27.done.mine), channel_id=1, source_target_pairs={{80,96},{81,97},{82,98},{83,99},{84,100},{85,101},{86,102},{87,103... | collective-permute-start | bytes 786440 | tf_op jit(solution)/shard_map/near13/ppermute | solution.py:361
  274.3 16.3 %collective-permute-start.42 = (f32[512,128]{1,0:T(8,128)S(1)}, f32[512,128]{1,0:T(8,128)S(1)}, u32[]{:S(2)}, u32[]{:S(2)}) collective-permute-start(f32[512,128]{1,0:T(8,128)S(1)} %near.27.done.mine), channel_id=1, source_target_pairs={{64,112},{65,113},{66,114},{67,115},{68,116},{69,117},{70,118},{71... | collective-permute-start | bytes 786440 | tf_op jit(solution)/shard_map/far13/ppermute | solution.py:366
  275.6 20.4 %collective-permute-start.41 = (f32[512,128]{1,0:T(8,128)S(1)}, f32[512,128]{1,0:T(8,128)S(1)}, u32[]{:S(2)}, u32[]{:S(2)}) collective-permute-start(f32[512,128]{1,0:T(8,128)S(1)} %near.27.done.mine), channel_id=1, source_target_pairs={{80,112},{81,113},{82,114},{83,115},{84,116},{85,117},{86,118},{87... | collective-permute-start | bytes 786440 | tf_op jit(solution)/shard_map/far13/ppermute | solution.py:365
  285.2 16.1 %collective-permute-start.40 = (f32[512,128]{1,0:T(8,128)S(1)}, f32[512,128]{1,0:T(8,128)S(1)}, u32[]{:S(2)}, u32[]{:S(2)}) collective-permute-start(f32[512,128]{1,0:T(8,128)S(1)} %near.28.done.mine), channel_id=1, source_target_pairs={{96,112},{97,113},{98,114},{99,115},{100,116},{101,117},{102,118},... | collective-permute-start | bytes 786440 | tf_op jit(solution)/shard_map/near14/ppermute | solution.py:361
  (2 other events, 5.0 us)
Sparse Core Ops, SparseCore 0:
  27.1 58.7 all-gather.5
  87.6 92.2 all-gather.3

commit v2 on v1

--- a/solution.py
+++ b/solution.py
@@ -176,7 +176,7 @@
             def mul(ds):
                 out[ds] = cur[ds] - mmw(nearh[ds], nearl[ds], w)
 
-            rows_loop(out.shape[0], mul)
+            rows_loop(out.shape[0], mul, out.shape[0])
             if keep:
                 k = nth(row, 7)
                 rest[1][k] = got[...]
@@ -257,15 +257,18 @@
 
     def kernel(row, hi, lo, store, acc, xb, xa, out, last):
         out[...] = acc[...]
+        fresh = nth(row, 2) > 0
+        kb = nth(row, 3)
+        ka = nth(row, 4)
 
         def one(k, _):
             last[...] = store[k]
 
-            @pl.when((nth(row, 2) > 0) & (nth(row, 3) == k))
+            @pl.when(fresh & (kb == k))
             def _():
                 last[...] = xb[...]
 
-            @pl.when((nth(row, 2) > 0) & (nth(row, 4) == k))
+            @pl.when(fresh & (ka == k))
             def _():
                 last[...] = xa[...]
 
@@ -274,7 +277,7 @@
             def mul(ds):
                 out[ds] = out[ds] - mmw(hi[k, ds], lo[k, ds], w)
 
-            rows_loop(nb, mul)
+            rows_loop(nb, mul, nb)
             return 0
 
         lax.fori_loop(0, count, one, 0)
@@ -331,17 +334,17 @@
     for t in range(C - 1):
         q = (p - t) % R
         i = t + q
-        kA = i - 2 * q + 1
-        kB = kA + 1
-        inwin = (q >= 2) & (q <= 4)
+        kB = i - 2 * q + 2
+        kA = kB + 1
+        inwin = (q >= 2) & (q <= 5)
         first = t + 1 < R
         top_k = R - 1 if first else C - 1
         rows.append(sublanes(
             jnp.clip(kB, 0, top_k),
             jnp.clip(kA, 0, top_k),
             inwin,
-            jnp.where(kB >= 0, jnp.minimum(kB, R), R),
-            jnp.where(kA >= 0, jnp.minimum(kA, R), R),
+            jnp.where((kB >= 0) & (q <= 4), jnp.minimum(kB, R), R),
+            jnp.where((kA >= 0) & (q >= 3), jnp.minimum(kA, R), R),
             p if first else R + p,
             p == (t + 1) % R,
             min(t, R - 1),
@@ -360,7 +363,7 @@
         with jax.named_scope(f"near{t}"):
             P1 = lax.ppermute(mine, "row", [(s, (s + 1) % R)])
         B = [((t - j) % R, (t + 2 + j) % R) for j in range(3) if t - j >= 0 and t + 2 + j < C]
-        A = [((t - j) % R, (t + 1 + j) % R) for j in range(1, 4) if t - j >= 0 and t + 1 + j < C]
+        A = [((t - j) % R, (t + 3 + j) % R) for j in range(3) if t - j >= 0 and t + 3 + j < C]
         with jax.named_scope(f"far{t}"):
             XB = lax.ppermute(mine, "row", B) if B else zero
             XA = lax.ppermute(mine, "row", A) if A else zero

time: 311 us -> 300 us (0.965)
  waiting for transfers between devices: 175 us -> 169 us
  starting transfers between devices: 62.8 us -> 59.1 us
    ppermute x14, waiting for transfers between devices: 29 us -> 4.17 us  [on_device(): XB = lax.ppermute(mine, 'row', B) if B else zero]
    ppermute x13, waiting for transfers between devices: 81.6 us -> 96.7 us  [on_device(): XA = lax.ppermute(mine, 'row', A) if A else zero]
    ppermute x13, starting transfers between devices: 21.2 us -> 15.3 us  [on_device(): XA = lax.ppermute(mine, 'row', A) if A else zero]
    pallas_call x1, Pallas kernels: 9.41 us -> 4.89 us  [bulk_call(): pl.pallas_call(kernel, out_shape=jax.ShapeDtypeStruct(acc.shape, F32), in...]
    ppermute x15, waiting for transfers between devices: 6 us -> 10 us  [on_device(): P1 = lax.ppermute(mine, 'row', [(s, (s + 1) % R)])]
    pallas_call x13, Pallas kernels: 15 us -> 18.5 us  [far_call(): pl.pallas_call(kernel, out_shape=tuple(outs), in_specs=[vspec(), aspec()]...]
  transfers between devices with their start and end apart: 46 -> 46, of which waited for: 19 -> 13; matrix products, arithmetic and copies ran while one was open for 2% -> 2% of each run, Pallas kernels for 12% -> 12%
where the time goes in v2:
time: 300 us; the launch traced here: 299 us
  waiting for transfers between devices  169 us (56%)
  starting transfers between devices  59.1 us (20%)
  Pallas kernels  38 us (13%)
  local copies, waits for them, and re-layouts  16.4 us (5%)
  between operations  14.3 us (5%)
    ppermute x13, waiting for transfers between devices, on_device(): XA = lax.ppermute(mine, 'row', A) if A else zero  96.7 us
    all_gather x1, waiting for transfers between devices, on_device(): g0 = lax.all_gather(u0, 'col', axis=0, tiled=False).reshape(2, R, half, nb)  35.8 us
    ppermute x14, starting transfers between devices, on_device(): XB = lax.ppermute(mine, 'row', B) if B else zero  18.6 us
    pallas_call x13, Pallas kernels, far_call(): pl.pallas_call(kernel, out_shape=tuple(outs), in_specs=[vspec(), aspec()]...  18.5 us
    ppermute x13, starting transfers between devices, on_device(): XA = lax.ppermute(mine, 'row', A) if A else zero  15.3 us
    ppermute x15, starting transfers between devices, on_device(): P1 = lax.ppermute(mine, 'row', [(s, (s + 1) % R)])  12.7 us
    ppermute x1, waiting for transfers between devices, on_device(): moved = lax.ppermute(top[half:], 'col', [(i, i + R) for i in range(R)])  11.4 us
    unnamed x9, local copies, waits for them, and re-layouts  10.8 us
  transfers between devices with their start and end apart: 46, of which 13 were waited for; matrix products, arithmetic and copies ran while one was open for 2% of the time, Pallas kernels for 12%

profile of v2, /device:TPU:120, one launch (start us, length us, event | category | flops | bytes accessed | tf_op | source)
XLA Modules:
  0.0 298.7 jit_solution(17288958651541466468)
XLA Ops:
  6.6 1.6 copy-done.2
  9.7 4.9 %collective-permute-start = (f32[256,512]{1,0:T(8,128)}, f32[256,512]{1,0:T(8,128)S(1)}, u32[]{:S(2)}, u32[]{:S(2)}) collective-permute-start(f32[256,512]{1,0:T(8,128)} %slice_bitcast_fusion), channel_id=1, source_target_pairs={{0,8},{1,9},{2,10},{3,11},{4,12},{5,13},{6,14},{7,15},{16,24},{17,... | collective-permute-start | bytes 1572872 | tf_op jit(solution)/shard_map/ppermute | solution.py:318
  14.7 11.4 %collective-permute-done = f32[256,512]{1,0:T(8,128)S(1)} collective-permute-done((f32[256,512]{1,0:T(8,128)}, f32[256,512]{1,0:T(8,128)S(1)}, u32[]{:S(2)}, u32[]{:S(2)}) %collective-permute-start) | collective-permute-done | bytes 524320 | tf_op jit(solution)/shard_map/ppermute | solution.py:318
  29.2 7.4 %all-to-all-start = ((f32[16,64,128]{2,1,0:T(8,128)}), f32[16,64,128]{2,1,0:T(8,128)S(1)}, u32[]{:S(2)}, u32[]{:S(2)}) async-start(f32[16,64,128]{2,1,0:T(8,128)} %copy.43), calls=%async_computation | async-start | bytes 1048576 | tf_op jit(solution)/shard_map/all_to_all | solution.py:325
  38.0 10.8 %all-to-all-done = f32[16,64,128]{2,1,0:T(8,128)S(1)} async-done(((f32[16,64,128]{2,1,0:T(8,128)}), f32[16,64,128]{2,1,0:T(8,128)S(1)}, u32[]{:S(2)}, u32[]{:S(2)}) %all-to-all-start) | async-done | bytes 524320 | tf_op jit(solution)/shard_map/all_to_all | solution.py:325
  50.1 35.8 %all-gather.6.cloned.1.call-done = f32[4096,512]{1,0:T(8,128)} async-done(((f32[256,512]{1,0:T(8,128)}), f32[4096,512]{1,0:T(8,128)}) %all-gather.6.cloned.1.call-update) | async-done | bytes 8388624 | tf_op jit(solution)/shard_map/all_gather | solution.py:321
  85.9 3.4 %copy-done.1 = f32[4096,512]{1,0:T(8,128)S(1)} copy-done((f32[4096,512]{1,0:T(8,128)S(1)}, f32[4096,512]{1,0:T(8,128)}, u32[]{:S(2)}) %copy-start.1) | copy-done | bytes 8388632
  89.3 2.0 load.2
  91.3 2.1 prep.2
  99.1 1.3 collective-permute-start.10
  102.2 1.3 collective-permute-start.13
  103.5 1.3 collective-permute-start.12
  104.8 38.1 %collective-permute-done.10.xa = f32[512,128]{1,0:T(8,128)S(1)} collective-permute-done((f32[512,128]{1,0:T(8,128)S(1)}, f32[512,128]{1,0:T(8,128)S(1)}, u32[]{:S(2)}, u32[]{:S(2)}) %collective-permute-start.10) | collective-permute-done | bytes 262176 | tf_op jit(solution)/shard_map/far2/ppermute | solution.py:369
  142.9 2.2 far.15
  146.0 1.3 collective-permute-start.16
  148.6 17.6 %collective-permute-done.13.xa = f32[512,128]{1,0:T(8,128)S(1)} collective-permute-done((f32[512,128]{1,0:T(8,128)S(1)}, f32[512,128]{1,0:T(8,128)S(1)}, u32[]{:S(2)}, u32[]{:S(2)}) %collective-permute-start.13) | collective-permute-done | bytes 262176 | tf_op jit(solution)/shard_map/far3/ppermute | solution.py:369
  166.2 2.2 far.16
  171.3 16.0 %collective-permute-done.16.xa = f32[512,128]{1,0:T(8,128)S(1)} collective-permute-done((f32[512,128]{1,0:T(8,128)S(1)}, f32[512,128]{1,0:T(8,128)S(1)}, u32[]{:S(2)}, u32[]{:S(2)}) %collective-permute-start.16) | collective-permute-done | bytes 262176 | tf_op jit(solution)/shard_map/far4/ppermute | solution.py:369
  187.3 2.2 far.17
  189.7 1.3 collective-permute-start.17
  191.7 1.6 collective-permute-start.20
  193.3 2.2 far.18
  195.5 4.0 %collective-permute-done.17.got = f32[512,128]{1,0:T(8,128)S(1)} collective-permute-done((f32[512,128]{1,0:T(8,128)S(1)}, f32[512,128]{1,0:T(8,128)S(1)}, u32[]{:S(2)}, u32[]{:S(2)}) %collective-permute-start.17) | collective-permute-done | bytes 262176 | tf_op jit(solution)/shard_map/near6/ppermute | solution.py:364
  200.2 2.0 collective-permute-start.22
  202.2 2.0 collective-permute-start.25
  204.2 4.0 %collective-permute-start.24 = (f32[512,128]{1,0:T(8,128)S(1)}, f32[512,128]{1,0:T(8,128)}, u32[]{:S(2)}, u32[]{:S(2)}) collective-permute-start(f32[512,128]{1,0:T(8,128)S(1)} %get-tuple-element.120.mine), channel_id=1, source_target_pairs={{112,16},{96,32},{80,48},{113,17},{97,33},{81,49},{114,18},{98,34}... | collective-permute-start | bytes 786440 | tf_op jit(solution)/shard_map/far7/ppermute | solution.py:368
  208.2 5.8 %copy-done = f32[16,512,512]{2,1,0:T(8,128)S(1)} copy-done((f32[16,512,512]{2,1,0:T(8,128)S(1)}, f32[16,512,512]{2,1,0:T(8,128)}, u32[]{:S(2)}) %copy-start) | copy-done | bytes 16777240
  213.9 2.8 load.3
  216.7 4.9 %bulk.1.acc = f32[512,128]{1,0:T(8,128)S(1)} custom-call(s32[8,128]{1,0:T(8,128)S(1)} %broadcast_in_dim.45.row, bf16[16,512,512]{2,1,0:T(8,128)(2,1)S(1)} %get-tuple-element.123.hi, bf16[16,512,512]{2,1,0:T(8,128)(2,1)S(1)} %get-tuple-element.124.lo, f32[9,512,128]{2,1,0:T(8,128)S(1)} %get-tuple-element.125.store, f32[512,128]{1,0:T(8,128)S(1)} %bitcast.114, ...), custom_call_target="tpu_custom_call" | custom-call | tf_op jit(solution)/shard_map/bulk/pallas_call | solution.py:285
  221.6 2.0 prep.3
  225.5 1.3 collective-permute-start.28
  226.9 1.3 collective-permute-start.27
  230.4 1.5 collective-permute-start.31
  231.9 1.3 collective-permute-start.30
  233.2 2.2 collective-permute-done.27.xb
  239.7 1.3 collective-permute-start.37
  241.0 1.3 collective-permute-start.36
  242.3 13.0 %collective-permute-done.34.xa = f32[512,128]{1,0:T(8,128)S(1)} collective-permute-done((f32[512,128]{1,0:T(8,128)S(1)}, f32[512,128]{1,0:T(8,128)S(1)}, u32[]{:S(2)}, u32[]{:S(2)}) %collective-permute-start.34) | collective-permute-done | bytes 262176 | tf_op jit(solution)/shard_map/far10/ppermute | solution.py:369
  255.3 1.9 far.22
  258.2 1.3 collective-permute-start.40
  259.5 1.3 collective-permute-start.39
  260.8 4.0 %collective-permute-done.37.xa = f32[512,128]{1,0:T(8,128)S(1)} collective-permute-done((f32[512,128]{1,0:T(8,128)S(1)}, f32[512,128]{1,0:T(8,128)S(1)}, u32[]{:S(2)}, u32[]{:S(2)}) %collective-permute-start.37) | collective-permute-done | bytes 262176 | tf_op jit(solution)/shard_map/far11/ppermute | solution.py:369
  264.8 1.9 far.23
  269.0 8.0 %collective-permute-done.40.xa = f32[512,128]{1,0:T(8,128)S(1)} collective-permute-done((f32[512,128]{1,0:T(8,128)S(1)}, f32[512,128]{1,0:T(8,128)S(1)}, u32[]{:S(2)}, u32[]{:S(2)}) %collective-permute-start.40) | collective-permute-done | bytes 262176 | tf_op jit(solution)/shard_map/far12/ppermute | solution.py:369
  277.0 1.9 far.24
  280.5 1.9 collective-permute-done.42.xb
  282.5 1.9 far.25
  284.4 6.0 %collective-permute-done.41.got = f32[512,128]{1,0:T(8,128)S(1)} collective-permute-done((f32[512,128]{1,0:T(8,128)S(1)}, f32[512,128]{1,0:T(8,128)S(1)}, u32[]{:S(2)}, u32[]{:S(2)}) %collective-permute-start.41) | collective-permute-done | bytes 262176 | tf_op jit(solution)/shard_map/near14/ppermute | solution.py:364
  (135 shorter events, 35.6 us)
Async XLA Ops:
  6.5 79.4 %all-gather.6.cloned.1.call-start = ((), (), s32[]{:S(2)}) async-start(), calls=%async_computation.2 | async-start | bytes 8912896 | tf_op jit(solution)/shard_map/all_gather | solution.py:321
  9.7 16.4 %collective-permute-start = (f32[256,512]{1,0:T(8,128)}, f32[256,512]{1,0:T(8,128)S(1)}, u32[]{:S(2)}, u32[]{:S(2)}) collective-permute-start(f32[256,512]{1,0:T(8,128)} %slice_bitcast_fusion), channel_id=1, source_target_pairs={{0,8},{1,9},{2,10},{3,11},{4,12},{5,13},{6,14},{7,15},{16,24},{17,... | collective-permute-start | bytes 1572872 | tf_op jit(solution)/shard_map/ppermute | solution.py:318
  14.7 13.5 %copy-start.3 = (f32[64,2048]{1,0:T(8,128)S(1)}, f32[64,2048]{1,0:T(8,128)}, u32[]{:S(2)}) copy-start(f32[64,2048]{1,0:T(8,128)} %param.3) | copy-start | bytes 1572868
  27.0 181.1 %all-gather.4.cloned.1.call-start = ((), (), s32[]{:S(2)}) async-start(), calls=%async_computation.1 | async-start | bytes 17825792 | tf_op jit(solution)/shard_map/all_gather | solution.py:322
  29.2 19.6 %all-to-all-start = ((f32[16,64,128]{2,1,0:T(8,128)}), f32[16,64,128]{2,1,0:T(8,128)S(1)}, u32[]{:S(2)}, u32[]{:S(2)}) async-start(f32[16,64,128]{2,1,0:T(8,128)} %copy.43), calls=%async_computation | async-start | bytes 1048576 | tf_op jit(solution)/shard_map/all_to_all | solution.py:325
  93.3 2.3 collective-permute-start.1
  94.0 3.9 %collective-permute-start.3 = (f32[512,128]{1,0:T(8,128)S(1)}, f32[512,128]{1,0:T(8,128)S(1)}, u32[]{:S(2)}, u32[]{:S(2)}) collective-permute-start(f32[512,128]{1,0:T(8,128)S(1)} %broadcast_select_fusion.mine), channel_id=1, source_target_pairs={{0,32},{1,33},{2,34},{3,35},{4,36},{5,37},{6,38},{7,39},{8,40},{9,... | collective-permute-start | bytes 786440 | tf_op jit(solution)/shard_map/far0/ppermute | solution.py:368
  94.7 3.2 %collective-permute-start.4 = (f32[512,128]{1,0:T(8,128)S(1)}, f32[512,128]{1,0:T(8,128)S(1)}, u32[]{:S(2)}, u32[]{:S(2)}) collective-permute-start(f32[512,128]{1,0:T(8,128)S(1)} %broadcast_select_fusion.mine), channel_id=1, source_target_pairs={{0,48},{1,49},{2,50},{3,51},{4,52},{5,53},{6,54},{7,55},{8,56},{9,... | collective-permute-start | bytes 786440 | tf_op jit(solution)/shard_map/far0/ppermute | solution.py:369
  95.9 2.3 collective-permute-start.2
  96.5 4.5 %collective-permute-start.7 = (f32[512,128]{1,0:T(8,128)S(1)}, f32[512,128]{1,0:T(8,128)S(1)}, u32[]{:S(2)}, u32[]{:S(2)}) collective-permute-start(f32[512,128]{1,0:T(8,128)S(1)} %get-tuple-element.91.done.mine), channel_id=1, source_target_pairs={{16,64},{0,80},{17,65},{1,81},{18,66},{2,82},{19,67},{3,83},{20,68... | collective-permute-start | bytes 786440 | tf_op jit(solution)/shard_map/far1/ppermute | solution.py:369
  97.2 3.8 %collective-permute-start.6 = (f32[512,128]{1,0:T(8,128)S(1)}, f32[512,128]{1,0:T(8,128)S(1)}, u32[]{:S(2)}, u32[]{:S(2)}) collective-permute-start(f32[512,128]{1,0:T(8,128)S(1)} %get-tuple-element.91.done.mine), channel_id=1, source_target_pairs={{16,48},{0,64},{17,49},{1,65},{18,50},{2,66},{19,51},{3,67},{20,52... | collective-permute-start | bytes 786440 | tf_op jit(solution)/shard_map/far1/ppermute | solution.py:368
  98.4 2.9 collective-permute-start.5
  99.1 43.8 %collective-permute-start.10 = (f32[512,128]{1,0:T(8,128)S(1)}, f32[512,128]{1,0:T(8,128)S(1)}, u32[]{:S(2)}, u32[]{:S(2)}) collective-permute-start(f32[512,128]{1,0:T(8,128)S(1)} %get-tuple-element.95.done.mine), channel_id=1, source_target_pairs={{32,80},{16,96},{0,112},{33,81},{17,97},{1,113},{34,82},{18,98},{2... | collective-permute-start | bytes 786440 | tf_op jit(solution)/shard_map/far2/ppermute | solution.py:369
  100.4 42.5 %collective-permute-start.9 = (f32[512,128]{1,0:T(8,128)S(1)}, f32[512,128]{1,0:T(8,128)S(1)}, u32[]{:S(2)}, u32[]{:S(2)}) collective-permute-start(f32[512,128]{1,0:T(8,128)S(1)} %get-tuple-element.95.done.mine), channel_id=1, source_target_pairs={{32,64},{16,80},{0,96},{33,65},{17,81},{1,97},{34,66},{18,82},{2,9... | collective-permute-start | bytes 786440 | tf_op jit(solution)/shard_map/far2/ppermute | solution.py:368
  101.5 43.5 %collective-permute-start.8 = (f32[512,128]{1,0:T(8,128)S(1)}, f32[512,128]{1,0:T(8,128)S(1)}, u32[]{:S(2)}, u32[]{:S(2)}) collective-permute-start(f32[512,128]{1,0:T(8,128)S(1)} %get-tuple-element.100.done.mine), channel_id=1, source_target_pairs={{48,64},{49,65},{50,66},{51,67},{52,68},{53,69},{54,70},{55,71},{5... | collective-permute-start | bytes 786440 | tf_op jit(solution)/shard_map/near3/ppermute | solution.py:364
  102.2 64.0 %collective-permute-start.13 = (f32[512,128]{1,0:T(8,128)S(1)}, f32[512,128]{1,0:T(8,128)S(1)}, u32[]{:S(2)}, u32[]{:S(2)}) collective-permute-start(f32[512,128]{1,0:T(8,128)S(1)} %get-tuple-element.100.done.mine), channel_id=1, source_target_pairs={{48,96},{32,112},{16,0},{49,97},{33,113},{17,1},{50,98},{34,114},{... | collective-permute-start | bytes 786440 | tf_op jit(solution)/shard_map/far3/ppermute | solution.py:369
  103.5 62.7 %collective-permute-start.12 = (f32[512,128]{1,0:T(8,128)S(1)}, f32[512,128]{1,0:T(8,128)S(1)}, u32[]{:S(2)}, u32[]{:S(2)}) collective-permute-start(f32[512,128]{1,0:T(8,128)S(1)} %get-tuple-element.100.done.mine), channel_id=1, source_target_pairs={{48,80},{32,96},{16,112},{49,81},{33,97},{17,113},{50,82},{34,98},... | collective-permute-start | bytes 786440 | tf_op jit(solution)/shard_map/far3/ppermute | solution.py:368
  145.3 23.1 %collective-permute-start.11 = (f32[512,128]{1,0:T(8,128)S(1)}, f32[512,128]{1,0:T(8,128)S(1)}, u32[]{:S(2)}, u32[]{:S(2)}) collective-permute-start(f32[512,128]{1,0:T(8,128)S(1)} %get-tuple-element.105.done.mine), channel_id=1, source_target_pairs={{64,80},{65,81},{66,82},{67,83},{68,84},{69,85},{70,86},{71,87},{7... | collective-permute-start | bytes 786440 | tf_op jit(solution)/shard_map/near4/ppermute | solution.py:364
  146.0 41.3 %collective-permute-start.16 = (f32[512,128]{1,0:T(8,128)S(1)}, f32[512,128]{1,0:T(8,128)S(1)}, u32[]{:S(2)}, u32[]{:S(2)}) collective-permute-start(f32[512,128]{1,0:T(8,128)S(1)} %get-tuple-element.105.done.mine), channel_id=1, source_target_pairs={{64,112},{48,0},{32,16},{65,113},{49,1},{33,17},{66,114},{50,2},{3... | collective-permute-start | bytes 786440 | tf_op jit(solution)/shard_map/far4/ppermute | solution.py:369
  147.3 40.0 %collective-permute-start.15 = (f32[512,128]{1,0:T(8,128)S(1)}, f32[512,128]{1,0:T(8,128)S(1)}, u32[]{:S(2)}, u32[]{:S(2)}) collective-permute-start(f32[512,128]{1,0:T(8,128)S(1)} %get-tuple-element.105.done.mine), channel_id=1, source_target_pairs={{64,96},{48,112},{32,0},{65,97},{49,113},{33,1},{66,98},{50,114},{... | collective-permute-start | bytes 786440 | tf_op jit(solution)/shard_map/far4/ppermute | solution.py:368
  168.6 20.8 %collective-permute-start.14 = (f32[512,128]{1,0:T(8,128)S(1)}, f32[512,128]{1,0:T(8,128)S(1)}, u32[]{:S(2)}, u32[]{:S(2)}) collective-permute-start(f32[512,128]{1,0:T(8,128)S(1)} %get-tuple-element.110.done.mine), channel_id=1, source_target_pairs={{80,96},{81,97},{82,98},{83,99},{84,100},{85,101},{86,102},{87,103... | collective-permute-start | bytes 786440 | tf_op jit(solution)/shard_map/near5/ppermute | solution.py:364
  169.3 24.0 %collective-permute-start.19 = (f32[512,128]{1,0:T(8,128)S(1)}, f32[512,128]{1,0:T(8,128)S(1)}, u32[]{:S(2)}, u32[]{:S(2)}) collective-permute-start(f32[512,128]{1,0:T(8,128)S(1)} %get-tuple-element.110.done.mine), channel_id=1, source_target_pairs={{80,0},{64,16},{48,32},{81,1},{65,17},{49,33},{82,2},{66,18},{50,3... | collective-permute-start | bytes 786440 | tf_op jit(solution)/shard_map/far5/ppermute | solution.py:369
  170.0 23.3 %collective-permute-start.18 = (f32[512,128]{1,0:T(8,128)S(1)}, f32[512,128]{1,0:T(8,128)S(1)}, u32[]{:S(2)}, u32[]{:S(2)}) collective-permute-start(f32[512,128]{1,0:T(8,128)S(1)} %get-tuple-element.110.done.mine), channel_id=1, source_target_pairs={{80,112},{64,0},{48,16},{81,113},{65,1},{49,17},{82,114},{66,2},{5... | collective-permute-start | bytes 786440 | tf_op jit(solution)/shard_map/far5/ppermute | solution.py:368
  189.7 9.8 %collective-permute-start.17 = (f32[512,128]{1,0:T(8,128)S(1)}, f32[512,128]{1,0:T(8,128)S(1)}, u32[]{:S(2)}, u32[]{:S(2)}) collective-permute-start(f32[512,128]{1,0:T(8,128)S(1)} %get-tuple-element.115.done.mine), channel_id=1, source_target_pairs={{96,112},{97,113},{98,114},{99,115},{100,116},{101,117},{102,118},... | collective-permute-start | bytes 786440 | tf_op jit(solution)/shard_map/near6/ppermute | solution.py:364
  191.0 25.7 %collective-permute-start.21 = (f32[512,128]{1,0:T(8,128)S(1)}, f32[512,128]{1,0:T(8,128)S(1)}, u32[]{:S(2)}, u32[]{:S(2)}) collective-permute-start(f32[512,128]{1,0:T(8,128)S(1)} %get-tuple-element.115.done.mine), channel_id=1, source_target_pairs={{96,16},{80,32},{64,48},{97,17},{81,33},{65,49},{98,18},{82,34},{6... | collective-permute-start | bytes 786440 | tf_op jit(solution)/shard_map/far6/ppermute | solution.py:369
  191.7 25.0 %collective-permute-start.20 = (f32[512,128]{1,0:T(8,128)S(1)}, f32[512,128]{1,0:T(8,128)}, u32[]{:S(2)}, u32[]{:S(2)}) collective-permute-start(f32[512,128]{1,0:T(8,128)S(1)} %get-tuple-element.115.done.mine), channel_id=1, source_target_pairs={{96,0},{80,16},{64,32},{97,1},{81,17},{65,33},{98,2},{82,18},{66,3... | collective-permute-start | bytes 786440 | tf_op jit(solution)/shard_map/far6/ppermute | solution.py:368
  200.2 23.5 %collective-permute-start.22 = (f32[512,128]{1,0:T(8,128)S(1)}, f32[512,128]{1,0:T(8,128)}, u32[]{:S(2)}, u32[]{:S(2)}) collective-permute-start(f32[512,128]{1,0:T(8,128)S(1)} %get-tuple-element.120.mine), channel_id=1, source_target_pairs={{112,0},{113,1},{114,2},{115,3},{116,4},{117,5},{118,6},{119,7},{1... | collective-permute-start | bytes 786440 | tf_op jit(solution)/shard_map/near7/ppermute | solution.py:364
  202.2 26.0 %collective-permute-start.25 = (f32[512,128]{1,0:T(8,128)S(1)}, f32[512,128]{1,0:T(8,128)}, u32[]{:S(2)}, u32[]{:S(2)}) collective-permute-start(f32[512,128]{1,0:T(8,128)S(1)} %get-tuple-element.120.mine), channel_id=1, source_target_pairs={{112,32},{96,48},{80,64},{113,33},{97,49},{81,65},{114,34},{98,50}... | collective-permute-start | bytes 786440 | tf_op jit(solution)/shard_map/far7/ppermute | solution.py:369
  204.2 24.0 %collective-permute-start.24 = (f32[512,128]{1,0:T(8,128)S(1)}, f32[512,128]{1,0:T(8,128)}, u32[]{:S(2)}, u32[]{:S(2)}) collective-permute-start(f32[512,128]{1,0:T(8,128)S(1)} %get-tuple-element.120.mine), channel_id=1, source_target_pairs={{112,16},{96,32},{80,48},{113,17},{97,33},{81,49},{114,18},{98,34}... | collective-permute-start | bytes 786440 | tf_op jit(solution)/shard_map/far7/ppermute | solution.py:368
  208.2 5.8 %copy-start = (f32[16,512,512]{2,1,0:T(8,128)S(1)}, f32[16,512,512]{2,1,0:T(8,128)}, u32[]{:S(2)}) copy-start(f32[16,512,512]{2,1,0:T(8,128)} %all-gather.4.cloned.1.call-done) | copy-start | bytes 50331652
  224.9 4.6 %collective-permute-start.23 = (f32[512,128]{1,0:T(8,128)S(1)}, f32[512,128]{1,0:T(8,128)S(1)}, u32[]{:S(2)}, u32[]{:S(2)}) collective-permute-start(f32[512,128]{1,0:T(8,128)S(1)} %near.22.done.mine), channel_id=1, source_target_pairs={{0,16},{1,17},{2,18},{3,19},{4,20},{5,21},{6,22},{7,23},{8,24},{9,... | collective-permute-start | bytes 786440 | tf_op jit(solution)/shard_map/near8/ppermute | solution.py:364
  225.5 7.7 %collective-permute-start.28 = (f32[512,128]{1,0:T(8,128)S(1)}, f32[512,128]{1,0:T(8,128)S(1)}, u32[]{:S(2)}, u32[]{:S(2)}) collective-permute-start(f32[512,128]{1,0:T(8,128)S(1)} %near.22.done.mine), channel_id=1, source_target_pairs={{0,48},{112,64},{96,80},{1,49},{113,65},{97,81},{2,50},{114,66},{9... | collective-permute-start | bytes 786440 | tf_op jit(solution)/shard_map/far8/ppermute | solution.py:369
  226.9 8.6 %collective-permute-start.27 = (f32[512,128]{1,0:T(8,128)S(1)}, f32[512,128]{1,0:T(8,128)S(1)}, u32[]{:S(2)}, u32[]{:S(2)}) collective-permute-start(f32[512,128]{1,0:T(8,128)S(1)} %near.22.done.mine), channel_id=1, source_target_pairs={{0,32},{112,48},{96,64},{1,33},{113,49},{97,65},{2,34},{114,50},{9... | collective-permute-start | bytes 786440 | tf_op jit(solution)/shard_map/far8/ppermute | solution.py:368
  229.7 5.9 %collective-permute-start.26 = (f32[512,128]{1,0:T(8,128)S(1)}, f32[512,128]{1,0:T(8,128)S(1)}, u32[]{:S(2)}, u32[]{:S(2)}) collective-permute-start(f32[512,128]{1,0:T(8,128)S(1)} %near.23.done.mine), channel_id=1, source_target_pairs={{16,32},{17,33},{18,34},{19,35},{20,36},{21,37},{22,38},{23,39},{2... | collective-permute-start | bytes 786440 | tf_op jit(solution)/shard_map/near9/ppermute | solution.py:364
  230.4 8.2 %collective-permute-start.31 = (f32[512,128]{1,0:T(8,128)S(1)}, f32[512,128]{1,0:T(8,128)S(1)}, u32[]{:S(2)}, u32[]{:S(2)}) collective-permute-start(f32[512,128]{1,0:T(8,128)S(1)} %near.23.done.mine), channel_id=1, source_target_pairs={{16,64},{0,80},{112,96},{17,65},{1,81},{113,97},{18,66},{2,82},{11... | collective-permute-start | bytes 786440 | tf_op jit(solution)/shard_map/far9/ppermute | solution.py:369
  231.9 6.6 %collective-permute-start.30 = (f32[512,128]{1,0:T(8,128)S(1)}, f32[512,128]{1,0:T(8,128)S(1)}, u32[]{:S(2)}, u32[]{:S(2)}) collective-permute-start(f32[512,128]{1,0:T(8,128)S(1)} %near.23.done.mine), channel_id=1, source_target_pairs={{16,48},{0,64},{112,80},{17,49},{1,65},{113,81},{18,50},{2,66},{11... | collective-permute-start | bytes 786440 | tf_op jit(solution)/shard_map/far9/ppermute | solution.py:368
  235.9 2.9 collective-permute-start.29
  236.5 18.8 %collective-permute-start.34 = (f32[512,128]{1,0:T(8,128)S(1)}, f32[512,128]{1,0:T(8,128)S(1)}, u32[]{:S(2)}, u32[]{:S(2)}) collective-permute-start(f32[512,128]{1,0:T(8,128)S(1)} %near.24.done.mine), channel_id=1, source_target_pairs={{32,80},{16,96},{0,112},{33,81},{17,97},{1,113},{34,82},{18,98},{2... | collective-permute-start | bytes 786440 | tf_op jit(solution)/shard_map/far10/ppermute | solution.py:369
  237.8 17.5 %collective-permute-start.33 = (f32[512,128]{1,0:T(8,128)S(1)}, f32[512,128]{1,0:T(8,128)S(1)}, u32[]{:S(2)}, u32[]{:S(2)}) collective-permute-start(f32[512,128]{1,0:T(8,128)S(1)} %near.24.done.mine), channel_id=1, source_target_pairs={{32,64},{16,80},{0,96},{33,65},{17,81},{1,97},{34,66},{18,82},{2,9... | collective-permute-start | bytes 786440 | tf_op jit(solution)/shard_map/far10/ppermute | solution.py:368
  239.0 18.3 %collective-permute-start.32 = (f32[512,128]{1,0:T(8,128)S(1)}, f32[512,128]{1,0:T(8,128)S(1)}, u32[]{:S(2)}, u32[]{:S(2)}) collective-permute-start(f32[512,128]{1,0:T(8,128)S(1)} %near.25.done.mine), channel_id=1, source_target_pairs={{48,64},{49,65},{50,66},{51,67},{52,68},{53,69},{54,70},{55,71},{5... | collective-permute-start | bytes 786440 | tf_op jit(solution)/shard_map/near11/ppermute | solution.py:364
  239.7 25.1 %collective-permute-start.37 = (f32[512,128]{1,0:T(8,128)S(1)}, f32[512,128]{1,0:T(8,128)S(1)}, u32[]{:S(2)}, u32[]{:S(2)}) collective-permute-start(f32[512,128]{1,0:T(8,128)S(1)} %near.25.done.mine), channel_id=1, source_target_pairs={{48,96},{32,112},{49,97},{33,113},{50,98},{34,114},{51,99},{35,115... | collective-permute-start | bytes 786440 | tf_op jit(solution)/shard_map/far11/ppermute | solution.py:369
  241.0 23.8 %collective-permute-start.36 = (f32[512,128]{1,0:T(8,128)S(1)}, f32[512,128]{1,0:T(8,128)S(1)}, u32[]{:S(2)}, u32[]{:S(2)}) collective-permute-start(f32[512,128]{1,0:T(8,128)S(1)} %near.25.done.mine), channel_id=1, source_target_pairs={{48,80},{32,96},{16,112},{49,81},{33,97},{17,113},{50,82},{34,98},... | collective-permute-start | bytes 786440 | tf_op jit(solution)/shard_map/far11/ppermute | solution.py:368
  257.5 9.2 %collective-permute-start.35 = (f32[512,128]{1,0:T(8,128)S(1)}, f32[512,128]{1,0:T(8,128)S(1)}, u32[]{:S(2)}, u32[]{:S(2)}) collective-permute-start(f32[512,128]{1,0:T(8,128)S(1)} %near.26.done.mine), channel_id=1, source_target_pairs={{64,80},{65,81},{66,82},{67,83},{68,84},{69,85},{70,86},{71,87},{7... | collective-permute-start | bytes 786440 | tf_op jit(solution)/shard_map/near12/ppermute | solution.py:364
  258.2 18.8 %collective-permute-start.40 = (f32[512,128]{1,0:T(8,128)S(1)}, f32[512,128]{1,0:T(8,128)S(1)}, u32[]{:S(2)}, u32[]{:S(2)}) collective-permute-start(f32[512,128]{1,0:T(8,128)S(1)} %near.26.done.mine), channel_id=1, source_target_pairs={{64,112},{65,113},{66,114},{67,115},{68,116},{69,117},{70,118},{71... | collective-permute-start | bytes 786440 | tf_op jit(solution)/shard_map/far12/ppermute | solution.py:369
  259.5 17.5 %collective-permute-start.39 = (f32[512,128]{1,0:T(8,128)S(1)}, f32[512,128]{1,0:T(8,128)S(1)}, u32[]{:S(2)}, u32[]{:S(2)}) collective-permute-start(f32[512,128]{1,0:T(8,128)S(1)} %near.26.done.mine), channel_id=1, source_target_pairs={{64,96},{48,112},{65,97},{49,113},{66,98},{50,114},{67,99},{51,115... | collective-permute-start | bytes 786440 | tf_op jit(solution)/shard_map/far12/ppermute | solution.py:368
  267.0 12.0 %collective-permute-start.38 = (f32[512,128]{1,0:T(8,128)S(1)}, f32[512,128]{1,0:T(8,128)S(1)}, u32[]{:S(2)}, u32[]{:S(2)}) collective-permute-start(f32[512,128]{1,0:T(8,128)S(1)} %near.27.done.mine), channel_id=1, source_target_pairs={{80,96},{81,97},{82,98},{83,99},{84,100},{85,101},{86,102},{87,103... | collective-permute-start | bytes 786440 | tf_op jit(solution)/shard_map/near13/ppermute | solution.py:364
  267.7 14.8 %collective-permute-start.42 = (f32[512,128]{1,0:T(8,128)S(1)}, f32[512,128]{1,0:T(8,128)S(1)}, u32[]{:S(2)}, u32[]{:S(2)}) collective-permute-start(f32[512,128]{1,0:T(8,128)S(1)} %near.27.done.mine), channel_id=1, source_target_pairs={{80,112},{81,113},{82,114},{83,115},{84,116},{85,117},{86,118},{87... | collective-permute-start | bytes 786440 | tf_op jit(solution)/shard_map/far13/ppermute | solution.py:368
  279.2 11.2 %collective-permute-start.41 = (f32[512,128]{1,0:T(8,128)S(1)}, f32[512,128]{1,0:T(8,128)S(1)}, u32[]{:S(2)}, u32[]{:S(2)}) collective-permute-start(f32[512,128]{1,0:T(8,128)S(1)} %near.28.done.mine), channel_id=1, source_target_pairs={{96,112},{97,113},{98,114},{99,115},{100,116},{101,117},{102,118},... | collective-permute-start | bytes 786440 | tf_op jit(solution)/shard_map/near14/ppermute | solution.py:364
  (2 other events, 5.0 us)
Sparse Core Ops, SparseCore 0:
  27.1 58.7 all-gather.5
  87.6 92.2 all-gather.3

commit v3 on v2

--- a/solution.py
+++ b/solution.py
@@ -210,7 +210,9 @@
     def kernel(row, done, hi, lo, acc, cur, xb, xa, *rest):
         acc_out, cur_out = rest[-2:]
 
-        @pl.when(nth(row, 2) > 0)
+        ahead = nth(row, 2)
+
+        @pl.when(ahead > 0)
         def _():
             kb = nth(row, 0)
             ka = nth(row, 1)
@@ -218,10 +220,20 @@
             wb = wide(xb[...])
             wa = wide(xa[...])
 
-            def mul(ds):
-                acc_out[ds] = acc[ds] - (mmw(hi[kb, ds], lo[kb, ds], wb) + mmw(hi[ka, ds], lo[ka, ds], wa))
-
-            rows_loop(nb, mul)
+            @pl.when(ahead == 2)
+            def _():
+                def mul(ds):
+                    acc_out[ds] = acc[ds] - mmw(hi[kb, ds], lo[kb, ds], wb)
+
+                rows_loop(nb, mul)
+
+            @pl.when(ahead > 2)
+            def _():
+                def mul(ds):
+                    acc_out[ds] = acc[ds] - (mmw(hi[kb, ds], lo[kb, ds], wb) + mmw(hi[ka, ds], lo[ka, ds], wa))
+
+                rows_loop(nb, mul)
+
             a = wide(acc_out[...])
 
             def mul2(ds):
@@ -336,7 +348,7 @@
         i = t + q
         kB = i - 2 * q + 2
         kA = kB + 1
-        inwin = (q >= 2) & (q <= 5)
+        inwin = jnp.where((q >= 2) & (q <= 5), q, 0)
         first = t + 1 < R
         top_k = R - 1 if first else C - 1
         rows.append(sublanes(

time: 300 us -> 300 us (level)
  no operation moved by 1% of the time
where the time goes in v3:
time: 300 us; the launch traced here: 298 us
  waiting for transfers between devices  169 us (56%)
  starting transfers between devices  58.8 us (20%)
  Pallas kernels  37.7 us (13%)
  local copies, waits for them, and re-layouts  16.4 us (5%)
  between operations  14.3 us (5%)
    ppermute x13, waiting for transfers between devices, on_device(): XA = lax.ppermute(mine, 'row', A) if A else zero  96.4 us
    all_gather x1, waiting for transfers between devices, on_device(): g0 = lax.all_gather(u0, 'col', axis=0, tiled=False).reshape(2, R, half, nb)  35.9 us
    ppermute x14, starting transfers between devices, on_device(): XB = lax.ppermute(mine, 'row', B) if B else zero  18.3 us
    pallas_call x13, Pallas kernels, far_call(): pl.pallas_call(kernel, out_shape=tuple(outs), in_specs=[vspec(), aspec()]...  18.2 us
    ppermute x13, starting transfers between devices, on_device(): XA = lax.ppermute(mine, 'row', A) if A else zero  15.3 us
    ppermute x15, starting transfers between devices, on_device(): P1 = lax.ppermute(mine, 'row', [(s, (s + 1) % R)])  12.7 us
    ppermute x1, waiting for transfers between devices, on_device(): moved = lax.ppermute(top[half:], 'col', [(i, i + R) for i in range(R)])  11.4 us
    unnamed x9, local copies, waits for them, and re-layouts  10.8 us
  transfers between devices with their start and end apart: 46, of which 13 were waited for; matrix products, arithmetic and copies ran while one was open for 2% of the time, Pallas kernels for 12%

profile of v3, /device:TPU:120, one launch (start us, length us, event | category | flops | bytes accessed | tf_op | source)
XLA Modules:
  0.0 298.4 jit_solution(17850477039417718065)
XLA Ops:
  6.6 1.6 copy-done.2
  9.7 4.9 %collective-permute-start = (f32[256,512]{1,0:T(8,128)}, f32[256,512]{1,0:T(8,128)S(1)}, u32[]{:S(2)}, u32[]{:S(2)}) collective-permute-start(f32[256,512]{1,0:T(8,128)} %slice_bitcast_fusion), channel_id=1, source_target_pairs={{0,8},{1,9},{2,10},{3,11},{4,12},{5,13},{6,14},{7,15},{16,24},{17,... | collective-permute-start | bytes 1572872 | tf_op jit(solution)/shard_map/ppermute | solution.py:330
  14.7 11.4 %collective-permute-done = f32[256,512]{1,0:T(8,128)S(1)} collective-permute-done((f32[256,512]{1,0:T(8,128)}, f32[256,512]{1,0:T(8,128)S(1)}, u32[]{:S(2)}, u32[]{:S(2)}) %collective-permute-start) | collective-permute-done | bytes 524320 | tf_op jit(solution)/shard_map/ppermute | solution.py:330
  29.2 7.4 %all-to-all-start = ((f32[16,64,128]{2,1,0:T(8,128)}), f32[16,64,128]{2,1,0:T(8,128)S(1)}, u32[]{:S(2)}, u32[]{:S(2)}) async-start(f32[16,64,128]{2,1,0:T(8,128)} %copy.43), calls=%async_computation | async-start | bytes 1048576 | tf_op jit(solution)/shard_map/all_to_all | solution.py:337
  38.0 10.8 %all-to-all-done = f32[16,64,128]{2,1,0:T(8,128)S(1)} async-done(((f32[16,64,128]{2,1,0:T(8,128)}), f32[16,64,128]{2,1,0:T(8,128)S(1)}, u32[]{:S(2)}, u32[]{:S(2)}) %all-to-all-start) | async-done | bytes 524320 | tf_op jit(solution)/shard_map/all_to_all | solution.py:337
  50.0 35.9 %all-gather.6.cloned.1.call-done = f32[4096,512]{1,0:T(8,128)} async-done(((f32[256,512]{1,0:T(8,128)}), f32[4096,512]{1,0:T(8,128)}) %all-gather.6.cloned.1.call-update) | async-done | bytes 8388624 | tf_op jit(solution)/shard_map/all_gather | solution.py:333
  85.9 3.4 %copy-done.1 = f32[4096,512]{1,0:T(8,128)S(1)} copy-done((f32[4096,512]{1,0:T(8,128)S(1)}, f32[4096,512]{1,0:T(8,128)}, u32[]{:S(2)}) %copy-start.1) | copy-done | bytes 8388632
  89.3 2.0 load.2
  91.3 2.1 prep.2
  99.1 1.3 collective-permute-start.10
  102.2 1.3 collective-permute-start.13
  103.5 1.3 collective-permute-start.12
  104.8 38.0 %collective-permute-done.10.xa = f32[512,128]{1,0:T(8,128)S(1)} collective-permute-done((f32[512,128]{1,0:T(8,128)S(1)}, f32[512,128]{1,0:T(8,128)S(1)}, u32[]{:S(2)}, u32[]{:S(2)}) %collective-permute-start.10) | collective-permute-done | bytes 262176 | tf_op jit(solution)/shard_map/far2/ppermute | solution.py:381
  142.9 2.2 far.15
  146.0 1.3 collective-permute-start.16
  147.3 1.3 collective-permute-start.15
  148.6 17.6 %collective-permute-done.13.xa = f32[512,128]{1,0:T(8,128)S(1)} collective-permute-done((f32[512,128]{1,0:T(8,128)S(1)}, f32[512,128]{1,0:T(8,128)S(1)}, u32[]{:S(2)}, u32[]{:S(2)}) %collective-permute-start.13) | collective-permute-done | bytes 262176 | tf_op jit(solution)/shard_map/far3/ppermute | solution.py:381
  166.2 2.2 far.16
  171.3 16.0 %collective-permute-done.16.xa = f32[512,128]{1,0:T(8,128)S(1)} collective-permute-done((f32[512,128]{1,0:T(8,128)S(1)}, f32[512,128]{1,0:T(8,128)S(1)}, u32[]{:S(2)}, u32[]{:S(2)}) %collective-permute-start.16) | collective-permute-done | bytes 262176 | tf_op jit(solution)/shard_map/far4/ppermute | solution.py:381
  187.3 2.4 far.17
  189.9 1.3 collective-permute-start.17
  191.9 1.4 collective-permute-start.20
  193.3 1.9 far.18
  195.2 4.5 %collective-permute-done.17.got = f32[512,128]{1,0:T(8,128)S(1)} collective-permute-done((f32[512,128]{1,0:T(8,128)S(1)}, f32[512,128]{1,0:T(8,128)S(1)}, u32[]{:S(2)}, u32[]{:S(2)}) %collective-permute-start.17) | collective-permute-done | bytes 262176 | tf_op jit(solution)/shard_map/near6/ppermute | solution.py:376
  200.3 2.0 collective-permute-start.22
  202.3 2.0 collective-permute-start.25
  204.3 3.9 %collective-permute-start.24 = (f32[512,128]{1,0:T(8,128)S(1)}, f32[512,128]{1,0:T(8,128)}, u32[]{:S(2)}, u32[]{:S(2)}) collective-permute-start(f32[512,128]{1,0:T(8,128)S(1)} %get-tuple-element.120.mine), channel_id=1, source_target_pairs={{112,16},{96,32},{80,48},{113,17},{97,33},{81,49},{114,18},{98,34}... | collective-permute-start | bytes 786440 | tf_op jit(solution)/shard_map/far7/ppermute | solution.py:380
  208.2 5.8 %copy-done = f32[16,512,512]{2,1,0:T(8,128)S(1)} copy-done((f32[16,512,512]{2,1,0:T(8,128)S(1)}, f32[16,512,512]{2,1,0:T(8,128)}, u32[]{:S(2)}) %copy-start) | copy-done | bytes 16777240
  214.0 2.8 load.3
  216.7 4.9 %bulk.1.acc = f32[512,128]{1,0:T(8,128)S(1)} custom-call(s32[8,128]{1,0:T(8,128)S(1)} %broadcast_in_dim.45.row, bf16[16,512,512]{2,1,0:T(8,128)(2,1)S(1)} %get-tuple-element.123.hi, bf16[16,512,512]{2,1,0:T(8,128)(2,1)S(1)} %get-tuple-element.124.lo, f32[9,512,128]{2,1,0:T(8,128)S(1)} %get-tuple-element.125.store, f32[512,128]{1,0:T(8,128)S(1)} %bitcast.114, ...), custom_call_target="tpu_custom_call" | custom-call | tf_op jit(solution)/shard_map/bulk/pallas_call | solution.py:297
  221.6 2.0 prep.3
  225.6 1.3 collective-permute-start.28
  226.9 1.3 collective-permute-start.27
  230.4 1.5 collective-permute-start.31
  231.9 1.3 collective-permute-start.30
  233.2 2.2 collective-permute-done.27.xb
  239.7 1.3 collective-permute-start.37
  241.0 1.3 collective-permute-start.36
  242.3 13.0 %collective-permute-done.34.xa = f32[512,128]{1,0:T(8,128)S(1)} collective-permute-done((f32[512,128]{1,0:T(8,128)S(1)}, f32[512,128]{1,0:T(8,128)S(1)}, u32[]{:S(2)}, u32[]{:S(2)}) %collective-permute-start.34) | collective-permute-done | bytes 262176 | tf_op jit(solution)/shard_map/far10/ppermute | solution.py:381
  255.3 2.0 far.22
  260.8 3.7 %collective-permute-done.37.xa = f32[512,128]{1,0:T(8,128)S(1)} collective-permute-done((f32[512,128]{1,0:T(8,128)S(1)}, f32[512,128]{1,0:T(8,128)S(1)}, u32[]{:S(2)}, u32[]{:S(2)}) %collective-permute-start.37) | collective-permute-done | bytes 262176 | tf_op jit(solution)/shard_map/far11/ppermute | solution.py:381
  264.5 2.0 far.23
  268.7 8.0 %collective-permute-done.40.xa = f32[512,128]{1,0:T(8,128)S(1)} collective-permute-done((f32[512,128]{1,0:T(8,128)S(1)}, f32[512,128]{1,0:T(8,128)S(1)}, u32[]{:S(2)}, u32[]{:S(2)}) %collective-permute-start.40) | collective-permute-done | bytes 262176 | tf_op jit(solution)/shard_map/far12/ppermute | solution.py:381
  276.7 1.9 far.24
  278.9 1.3 collective-permute-start.41
  280.2 1.9 collective-permute-done.42.xb
  282.2 1.7 far.25
  283.8 6.3 %collective-permute-done.41.got = f32[512,128]{1,0:T(8,128)S(1)} collective-permute-done((f32[512,128]{1,0:T(8,128)S(1)}, f32[512,128]{1,0:T(8,128)S(1)}, u32[]{:S(2)}, u32[]{:S(2)}) %collective-permute-start.41) | collective-permute-done | bytes 262176 | tf_op jit(solution)/shard_map/near14/ppermute | solution.py:376
  (135 shorter events, 35.6 us)
Async XLA Ops:
  6.5 79.4 %all-gather.6.cloned.1.call-start = ((), (), s32[]{:S(2)}) async-start(), calls=%async_computation.2 | async-start | bytes 8912896 | tf_op jit(solution)/shard_map/all_gather | solution.py:333
  9.7 16.4 %collective-permute-start = (f32[256,512]{1,0:T(8,128)}, f32[256,512]{1,0:T(8,128)S(1)}, u32[]{:S(2)}, u32[]{:S(2)}) collective-permute-start(f32[256,512]{1,0:T(8,128)} %slice_bitcast_fusion), channel_id=1, source_target_pairs={{0,8},{1,9},{2,10},{3,11},{4,12},{5,13},{6,14},{7,15},{16,24},{17,... | collective-permute-start | bytes 1572872 | tf_op jit(solution)/shard_map/ppermute | solution.py:330
  14.7 13.5 %copy-start.3 = (f32[64,2048]{1,0:T(8,128)S(1)}, f32[64,2048]{1,0:T(8,128)}, u32[]{:S(2)}) copy-start(f32[64,2048]{1,0:T(8,128)} %param.3) | copy-start | bytes 1572868
  27.0 181.2 %all-gather.4.cloned.1.call-start = ((), (), s32[]{:S(2)}) async-start(), calls=%async_computation.1 | async-start | bytes 17825792 | tf_op jit(solution)/shard_map/all_gather | solution.py:334
  29.2 19.6 %all-to-all-start = ((f32[16,64,128]{2,1,0:T(8,128)}), f32[16,64,128]{2,1,0:T(8,128)S(1)}, u32[]{:S(2)}, u32[]{:S(2)}) async-start(f32[16,64,128]{2,1,0:T(8,128)} %copy.43), calls=%async_computation | async-start | bytes 1048576 | tf_op jit(solution)/shard_map/all_to_all | solution.py:337
  93.3 2.3 collective-permute-start.1
  94.0 3.9 %collective-permute-start.3 = (f32[512,128]{1,0:T(8,128)S(1)}, f32[512,128]{1,0:T(8,128)S(1)}, u32[]{:S(2)}, u32[]{:S(2)}) collective-permute-start(f32[512,128]{1,0:T(8,128)S(1)} %broadcast_select_fusion.mine), channel_id=1, source_target_pairs={{0,32},{1,33},{2,34},{3,35},{4,36},{5,37},{6,38},{7,39},{8,40},{9,... | collective-permute-start | bytes 786440 | tf_op jit(solution)/shard_map/far0/ppermute | solution.py:380
  94.7 3.2 %collective-permute-start.4 = (f32[512,128]{1,0:T(8,128)S(1)}, f32[512,128]{1,0:T(8,128)S(1)}, u32[]{:S(2)}, u32[]{:S(2)}) collective-permute-start(f32[512,128]{1,0:T(8,128)S(1)} %broadcast_select_fusion.mine), channel_id=1, source_target_pairs={{0,48},{1,49},{2,50},{3,51},{4,52},{5,53},{6,54},{7,55},{8,56},{9,... | collective-permute-start | bytes 786440 | tf_op jit(solution)/shard_map/far0/ppermute | solution.py:381
  95.9 2.3 collective-permute-start.2
  96.5 4.5 %collective-permute-start.7 = (f32[512,128]{1,0:T(8,128)S(1)}, f32[512,128]{1,0:T(8,128)S(1)}, u32[]{:S(2)}, u32[]{:S(2)}) collective-permute-start(f32[512,128]{1,0:T(8,128)S(1)} %get-tuple-element.91.done.mine), channel_id=1, source_target_pairs={{16,64},{0,80},{17,65},{1,81},{18,66},{2,82},{19,67},{3,83},{20,68... | collective-permute-start | bytes 786440 | tf_op jit(solution)/shard_map/far1/ppermute | solution.py:381
  97.2 3.8 %collective-permute-start.6 = (f32[512,128]{1,0:T(8,128)S(1)}, f32[512,128]{1,0:T(8,128)S(1)}, u32[]{:S(2)}, u32[]{:S(2)}) collective-permute-start(f32[512,128]{1,0:T(8,128)S(1)} %get-tuple-element.91.done.mine), channel_id=1, source_target_pairs={{16,48},{0,64},{17,49},{1,65},{18,50},{2,66},{19,51},{3,67},{20,52... | collective-permute-start | bytes 786440 | tf_op jit(solution)/shard_map/far1/ppermute | solution.py:380
  98.4 2.9 collective-permute-start.5
  99.1 43.8 %collective-permute-start.10 = (f32[512,128]{1,0:T(8,128)S(1)}, f32[512,128]{1,0:T(8,128)S(1)}, u32[]{:S(2)}, u32[]{:S(2)}) collective-permute-start(f32[512,128]{1,0:T(8,128)S(1)} %get-tuple-element.95.done.mine), channel_id=1, source_target_pairs={{32,80},{16,96},{0,112},{33,81},{17,97},{1,113},{34,82},{18,98},{2... | collective-permute-start | bytes 786440 | tf_op jit(solution)/shard_map/far2/ppermute | solution.py:381
  100.4 42.5 %collective-permute-start.9 = (f32[512,128]{1,0:T(8,128)S(1)}, f32[512,128]{1,0:T(8,128)S(1)}, u32[]{:S(2)}, u32[]{:S(2)}) collective-permute-start(f32[512,128]{1,0:T(8,128)S(1)} %get-tuple-element.95.done.mine), channel_id=1, source_target_pairs={{32,64},{16,80},{0,96},{33,65},{17,81},{1,97},{34,66},{18,82},{2,9... | collective-permute-start | bytes 786440 | tf_op jit(solution)/shard_map/far2/ppermute | solution.py:380
  101.5 43.5 %collective-permute-start.8 = (f32[512,128]{1,0:T(8,128)S(1)}, f32[512,128]{1,0:T(8,128)S(1)}, u32[]{:S(2)}, u32[]{:S(2)}) collective-permute-start(f32[512,128]{1,0:T(8,128)S(1)} %get-tuple-element.100.done.mine), channel_id=1, source_target_pairs={{48,64},{49,65},{50,66},{51,67},{52,68},{53,69},{54,70},{55,71},{5... | collective-permute-start | bytes 786440 | tf_op jit(solution)/shard_map/near3/ppermute | solution.py:376
  102.2 64.0 %collective-permute-start.13 = (f32[512,128]{1,0:T(8,128)S(1)}, f32[512,128]{1,0:T(8,128)S(1)}, u32[]{:S(2)}, u32[]{:S(2)}) collective-permute-start(f32[512,128]{1,0:T(8,128)S(1)} %get-tuple-element.100.done.mine), channel_id=1, source_target_pairs={{48,96},{32,112},{16,0},{49,97},{33,113},{17,1},{50,98},{34,114},{... | collective-permute-start | bytes 786440 | tf_op jit(solution)/shard_map/far3/ppermute | solution.py:381
  103.5 62.7 %collective-permute-start.12 = (f32[512,128]{1,0:T(8,128)S(1)}, f32[512,128]{1,0:T(8,128)S(1)}, u32[]{:S(2)}, u32[]{:S(2)}) collective-permute-start(f32[512,128]{1,0:T(8,128)S(1)} %get-tuple-element.100.done.mine), channel_id=1, source_target_pairs={{48,80},{32,96},{16,112},{49,81},{33,97},{17,113},{50,82},{34,98},... | collective-permute-start | bytes 786440 | tf_op jit(solution)/shard_map/far3/ppermute | solution.py:380
  145.3 23.1 %collective-permute-start.11 = (f32[512,128]{1,0:T(8,128)S(1)}, f32[512,128]{1,0:T(8,128)S(1)}, u32[]{:S(2)}, u32[]{:S(2)}) collective-permute-start(f32[512,128]{1,0:T(8,128)S(1)} %get-tuple-element.105.done.mine), channel_id=1, source_target_pairs={{64,80},{65,81},{66,82},{67,83},{68,84},{69,85},{70,86},{71,87},{7... | collective-permute-start | bytes 786440 | tf_op jit(solution)/shard_map/near4/ppermute | solution.py:376
  146.0 41.3 %collective-permute-start.16 = (f32[512,128]{1,0:T(8,128)S(1)}, f32[512,128]{1,0:T(8,128)S(1)}, u32[]{:S(2)}, u32[]{:S(2)}) collective-permute-start(f32[512,128]{1,0:T(8,128)S(1)} %get-tuple-element.105.done.mine), channel_id=1, source_target_pairs={{64,112},{48,0},{32,16},{65,113},{49,1},{33,17},{66,114},{50,2},{3... | collective-permute-start | bytes 786440 | tf_op jit(solution)/shard_map/far4/ppermute | solution.py:381
  147.3 40.0 %collective-permute-start.15 = (f32[512,128]{1,0:T(8,128)S(1)}, f32[512,128]{1,0:T(8,128)S(1)}, u32[]{:S(2)}, u32[]{:S(2)}) collective-permute-start(f32[512,128]{1,0:T(8,128)S(1)} %get-tuple-element.105.done.mine), channel_id=1, source_target_pairs={{64,96},{48,112},{32,0},{65,97},{49,113},{33,1},{66,98},{50,114},{... | collective-permute-start | bytes 786440 | tf_op jit(solution)/shard_map/far4/ppermute | solution.py:380
  168.6 21.0 %collective-permute-start.14 = (f32[512,128]{1,0:T(8,128)S(1)}, f32[512,128]{1,0:T(8,128)S(1)}, u32[]{:S(2)}, u32[]{:S(2)}) collective-permute-start(f32[512,128]{1,0:T(8,128)S(1)} %get-tuple-element.110.done.mine), channel_id=1, source_target_pairs={{80,96},{81,97},{82,98},{83,99},{84,100},{85,101},{86,102},{87,103... | collective-permute-start | bytes 786440 | tf_op jit(solution)/shard_map/near5/ppermute | solution.py:376
  169.3 24.0 %collective-permute-start.19 = (f32[512,128]{1,0:T(8,128)S(1)}, f32[512,128]{1,0:T(8,128)S(1)}, u32[]{:S(2)}, u32[]{:S(2)}) collective-permute-start(f32[512,128]{1,0:T(8,128)S(1)} %get-tuple-element.110.done.mine), channel_id=1, source_target_pairs={{80,0},{64,16},{48,32},{81,1},{65,17},{49,33},{82,2},{66,18},{50,3... | collective-permute-start | bytes 786440 | tf_op jit(solution)/shard_map/far5/ppermute | solution.py:381
  170.0 23.3 %collective-permute-start.18 = (f32[512,128]{1,0:T(8,128)S(1)}, f32[512,128]{1,0:T(8,128)S(1)}, u32[]{:S(2)}, u32[]{:S(2)}) collective-permute-start(f32[512,128]{1,0:T(8,128)S(1)} %get-tuple-element.110.done.mine), channel_id=1, source_target_pairs={{80,112},{64,0},{48,16},{81,113},{65,1},{49,17},{82,114},{66,2},{5... | collective-permute-start | bytes 786440 | tf_op jit(solution)/shard_map/far5/ppermute | solution.py:380
  189.9 9.8 %collective-permute-start.17 = (f32[512,128]{1,0:T(8,128)S(1)}, f32[512,128]{1,0:T(8,128)S(1)}, u32[]{:S(2)}, u32[]{:S(2)}) collective-permute-start(f32[512,128]{1,0:T(8,128)S(1)} %get-tuple-element.115.done.mine), channel_id=1, source_target_pairs={{96,112},{97,113},{98,114},{99,115},{100,116},{101,117},{102,118},... | collective-permute-start | bytes 786440 | tf_op jit(solution)/shard_map/near6/ppermute | solution.py:376
  191.2 25.6 %collective-permute-start.21 = (f32[512,128]{1,0:T(8,128)S(1)}, f32[512,128]{1,0:T(8,128)S(1)}, u32[]{:S(2)}, u32[]{:S(2)}) collective-permute-start(f32[512,128]{1,0:T(8,128)S(1)} %get-tuple-element.115.done.mine), channel_id=1, source_target_pairs={{96,16},{80,32},{64,48},{97,17},{81,33},{65,49},{98,18},{82,34},{6... | collective-permute-start | bytes 786440 | tf_op jit(solution)/shard_map/far6/ppermute | solution.py:381
  191.9 24.9 %collective-permute-start.20 = (f32[512,128]{1,0:T(8,128)S(1)}, f32[512,128]{1,0:T(8,128)}, u32[]{:S(2)}, u32[]{:S(2)}) collective-permute-start(f32[512,128]{1,0:T(8,128)S(1)} %get-tuple-element.115.done.mine), channel_id=1, source_target_pairs={{96,0},{80,16},{64,32},{97,1},{81,17},{65,33},{98,2},{82,18},{66,3... | collective-permute-start | bytes 786440 | tf_op jit(solution)/shard_map/far6/ppermute | solution.py:380
  200.3 23.4 %collective-permute-start.22 = (f32[512,128]{1,0:T(8,128)S(1)}, f32[512,128]{1,0:T(8,128)}, u32[]{:S(2)}, u32[]{:S(2)}) collective-permute-start(f32[512,128]{1,0:T(8,128)S(1)} %get-tuple-element.120.mine), channel_id=1, source_target_pairs={{112,0},{113,1},{114,2},{115,3},{116,4},{117,5},{118,6},{119,7},{1... | collective-permute-start | bytes 786440 | tf_op jit(solution)/shard_map/near7/ppermute | solution.py:376
  202.3 25.9 %collective-permute-start.25 = (f32[512,128]{1,0:T(8,128)S(1)}, f32[512,128]{1,0:T(8,128)}, u32[]{:S(2)}, u32[]{:S(2)}) collective-permute-start(f32[512,128]{1,0:T(8,128)S(1)} %get-tuple-element.120.mine), channel_id=1, source_target_pairs={{112,32},{96,48},{80,64},{113,33},{97,49},{81,65},{114,34},{98,50}... | collective-permute-start | bytes 786440 | tf_op jit(solution)/shard_map/far7/ppermute | solution.py:381
  204.3 23.9 %collective-permute-start.24 = (f32[512,128]{1,0:T(8,128)S(1)}, f32[512,128]{1,0:T(8,128)}, u32[]{:S(2)}, u32[]{:S(2)}) collective-permute-start(f32[512,128]{1,0:T(8,128)S(1)} %get-tuple-element.120.mine), channel_id=1, source_target_pairs={{112,16},{96,32},{80,48},{113,17},{97,33},{81,49},{114,18},{98,34}... | collective-permute-start | bytes 786440 | tf_op jit(solution)/shard_map/far7/ppermute | solution.py:380
  208.2 5.8 %copy-start = (f32[16,512,512]{2,1,0:T(8,128)S(1)}, f32[16,512,512]{2,1,0:T(8,128)}, u32[]{:S(2)}) copy-start(f32[16,512,512]{2,1,0:T(8,128)} %all-gather.4.cloned.1.call-done) | copy-start | bytes 50331652
  224.9 4.6 %collective-permute-start.23 = (f32[512,128]{1,0:T(8,128)S(1)}, f32[512,128]{1,0:T(8,128)S(1)}, u32[]{:S(2)}, u32[]{:S(2)}) collective-permute-start(f32[512,128]{1,0:T(8,128)S(1)} %near.22.done.mine), channel_id=1, source_target_pairs={{0,16},{1,17},{2,18},{3,19},{4,20},{5,21},{6,22},{7,23},{8,24},{9,... | collective-permute-start | bytes 786440 | tf_op jit(solution)/shard_map/near8/ppermute | solution.py:376
  225.6 7.7 %collective-permute-start.28 = (f32[512,128]{1,0:T(8,128)S(1)}, f32[512,128]{1,0:T(8,128)S(1)}, u32[]{:S(2)}, u32[]{:S(2)}) collective-permute-start(f32[512,128]{1,0:T(8,128)S(1)} %near.22.done.mine), channel_id=1, source_target_pairs={{0,48},{112,64},{96,80},{1,49},{113,65},{97,81},{2,50},{114,66},{9... | collective-permute-start | bytes 786440 | tf_op jit(solution)/shard_map/far8/ppermute | solution.py:381
  226.9 8.5 %collective-permute-start.27 = (f32[512,128]{1,0:T(8,128)S(1)}, f32[512,128]{1,0:T(8,128)S(1)}, u32[]{:S(2)}, u32[]{:S(2)}) collective-permute-start(f32[512,128]{1,0:T(8,128)S(1)} %near.22.done.mine), channel_id=1, source_target_pairs={{0,32},{112,48},{96,64},{1,33},{113,49},{97,65},{2,34},{114,50},{9... | collective-permute-start | bytes 786440 | tf_op jit(solution)/shard_map/far8/ppermute | solution.py:380
  229.7 5.9 %collective-permute-start.26 = (f32[512,128]{1,0:T(8,128)S(1)}, f32[512,128]{1,0:T(8,128)S(1)}, u32[]{:S(2)}, u32[]{:S(2)}) collective-permute-start(f32[512,128]{1,0:T(8,128)S(1)} %near.23.done.mine), channel_id=1, source_target_pairs={{16,32},{17,33},{18,34},{19,35},{20,36},{21,37},{22,38},{23,39},{2... | collective-permute-start | bytes 786440 | tf_op jit(solution)/shard_map/near9/ppermute | solution.py:376
  230.4 8.2 %collective-permute-start.31 = (f32[512,128]{1,0:T(8,128)S(1)}, f32[512,128]{1,0:T(8,128)S(1)}, u32[]{:S(2)}, u32[]{:S(2)}) collective-permute-start(f32[512,128]{1,0:T(8,128)S(1)} %near.23.done.mine), channel_id=1, source_target_pairs={{16,64},{0,80},{112,96},{17,65},{1,81},{113,97},{18,66},{2,82},{11... | collective-permute-start | bytes 786440 | tf_op jit(solution)/shard_map/far9/ppermute | solution.py:381
  231.9 6.6 %collective-permute-start.30 = (f32[512,128]{1,0:T(8,128)S(1)}, f32[512,128]{1,0:T(8,128)S(1)}, u32[]{:S(2)}, u32[]{:S(2)}) collective-permute-start(f32[512,128]{1,0:T(8,128)S(1)} %near.23.done.mine), channel_id=1, source_target_pairs={{16,48},{0,64},{112,80},{17,49},{1,65},{113,81},{18,50},{2,66},{11... | collective-permute-start | bytes 786440 | tf_op jit(solution)/shard_map/far9/ppermute | solution.py:380
  235.9 2.9 collective-permute-start.29
  236.6 18.8 %collective-permute-start.34 = (f32[512,128]{1,0:T(8,128)S(1)}, f32[512,128]{1,0:T(8,128)S(1)}, u32[]{:S(2)}, u32[]{:S(2)}) collective-permute-start(f32[512,128]{1,0:T(8,128)S(1)} %near.24.done.mine), channel_id=1, source_target_pairs={{32,80},{16,96},{0,112},{33,81},{17,97},{1,113},{34,82},{18,98},{2... | collective-permute-start | bytes 786440 | tf_op jit(solution)/shard_map/far10/ppermute | solution.py:381
  237.9 17.5 %collective-permute-start.33 = (f32[512,128]{1,0:T(8,128)S(1)}, f32[512,128]{1,0:T(8,128)S(1)}, u32[]{:S(2)}, u32[]{:S(2)}) collective-permute-start(f32[512,128]{1,0:T(8,128)S(1)} %near.24.done.mine), channel_id=1, source_target_pairs={{32,64},{16,80},{0,96},{33,65},{17,81},{1,97},{34,66},{18,82},{2,9... | collective-permute-start | bytes 786440 | tf_op jit(solution)/shard_map/far10/ppermute | solution.py:380
  239.0 18.3 %collective-permute-start.32 = (f32[512,128]{1,0:T(8,128)S(1)}, f32[512,128]{1,0:T(8,128)S(1)}, u32[]{:S(2)}, u32[]{:S(2)}) collective-permute-start(f32[512,128]{1,0:T(8,128)S(1)} %near.25.done.mine), channel_id=1, source_target_pairs={{48,64},{49,65},{50,66},{51,67},{52,68},{53,69},{54,70},{55,71},{5... | collective-permute-start | bytes 786440 | tf_op jit(solution)/shard_map/near11/ppermute | solution.py:376
  239.7 24.8 %collective-permute-start.37 = (f32[512,128]{1,0:T(8,128)S(1)}, f32[512,128]{1,0:T(8,128)S(1)}, u32[]{:S(2)}, u32[]{:S(2)}) collective-permute-start(f32[512,128]{1,0:T(8,128)S(1)} %near.25.done.mine), channel_id=1, source_target_pairs={{48,96},{32,112},{49,97},{33,113},{50,98},{34,114},{51,99},{35,115... | collective-permute-start | bytes 786440 | tf_op jit(solution)/shard_map/far11/ppermute | solution.py:381
  241.0 23.5 %collective-permute-start.36 = (f32[512,128]{1,0:T(8,128)S(1)}, f32[512,128]{1,0:T(8,128)S(1)}, u32[]{:S(2)}, u32[]{:S(2)}) collective-permute-start(f32[512,128]{1,0:T(8,128)S(1)} %near.25.done.mine), channel_id=1, source_target_pairs={{48,80},{32,96},{16,112},{49,81},{33,97},{17,113},{50,82},{34,98},... | collective-permute-start | bytes 786440 | tf_op jit(solution)/shard_map/far11/ppermute | solution.py:380
  257.5 8.9 %collective-permute-start.35 = (f32[512,128]{1,0:T(8,128)S(1)}, f32[512,128]{1,0:T(8,128)S(1)}, u32[]{:S(2)}, u32[]{:S(2)}) collective-permute-start(f32[512,128]{1,0:T(8,128)S(1)} %near.26.done.mine), channel_id=1, source_target_pairs={{64,80},{65,81},{66,82},{67,83},{68,84},{69,85},{70,86},{71,87},{7... | collective-permute-start | bytes 786440 | tf_op jit(solution)/shard_map/near12/ppermute | solution.py:376
  258.2 18.5 %collective-permute-start.40 = (f32[512,128]{1,0:T(8,128)S(1)}, f32[512,128]{1,0:T(8,128)S(1)}, u32[]{:S(2)}, u32[]{:S(2)}) collective-permute-start(f32[512,128]{1,0:T(8,128)S(1)} %near.26.done.mine), channel_id=1, source_target_pairs={{64,112},{65,113},{66,114},{67,115},{68,116},{69,117},{70,118},{71... | collective-permute-start | bytes 786440 | tf_op jit(solution)/shard_map/far12/ppermute | solution.py:381
  259.5 17.2 %collective-permute-start.39 = (f32[512,128]{1,0:T(8,128)S(1)}, f32[512,128]{1,0:T(8,128)S(1)}, u32[]{:S(2)}, u32[]{:S(2)}) collective-permute-start(f32[512,128]{1,0:T(8,128)S(1)} %near.26.done.mine), channel_id=1, source_target_pairs={{64,96},{48,112},{65,97},{49,113},{66,98},{50,114},{67,99},{51,115... | collective-permute-start | bytes 786440 | tf_op jit(solution)/shard_map/far12/ppermute | solution.py:380
  266.7 12.0 %collective-permute-start.38 = (f32[512,128]{1,0:T(8,128)S(1)}, f32[512,128]{1,0:T(8,128)S(1)}, u32[]{:S(2)}, u32[]{:S(2)}) collective-permute-start(f32[512,128]{1,0:T(8,128)S(1)} %near.27.done.mine), channel_id=1, source_target_pairs={{80,96},{81,97},{82,98},{83,99},{84,100},{85,101},{86,102},{87,103... | collective-permute-start | bytes 786440 | tf_op jit(solution)/shard_map/near13/ppermute | solution.py:376
  267.4 14.8 %collective-permute-start.42 = (f32[512,128]{1,0:T(8,128)S(1)}, f32[512,128]{1,0:T(8,128)S(1)}, u32[]{:S(2)}, u32[]{:S(2)}) collective-permute-start(f32[512,128]{1,0:T(8,128)S(1)} %near.27.done.mine), channel_id=1, source_target_pairs={{80,112},{81,113},{82,114},{83,115},{84,116},{85,117},{86,118},{87... | collective-permute-start | bytes 786440 | tf_op jit(solution)/shard_map/far13/ppermute | solution.py:380
  278.9 11.2 %collective-permute-start.41 = (f32[512,128]{1,0:T(8,128)S(1)}, f32[512,128]{1,0:T(8,128)S(1)}, u32[]{:S(2)}, u32[]{:S(2)}) collective-permute-start(f32[512,128]{1,0:T(8,128)S(1)} %near.28.done.mine), channel_id=1, source_target_pairs={{96,112},{97,113},{98,114},{99,115},{100,116},{101,117},{102,118},... | collective-permute-start | bytes 786440 | tf_op jit(solution)/shard_map/near14/ppermute | solution.py:376
  (2 other events, 5.0 us)
Sparse Core Ops, SparseCore 0:
  27.1 58.7 all-gather.5
  87.6 92.2 all-gather.3
